TPU v7x, 256 devices: a whole 4x4x8 slice. The times are simulated.
256 devices in a mesh: gx: 8 (over y, x_hi), gy: 32 (over z, x_lo, core).
Axes of the slice: x: 4 (x_hi: 2, x_lo: 2; x = x_hi * 2 + x_lo), y: 4, z: 8, core: 2. Of those that a mesh axis runs over, the one named last changes fastest.
Arguments:
- species_means: bfloat16 [8, 64, 120, 1024], P(None, 'gy', None, 'gx'), may hold values from 0.19921875 to 5
- zonal_edge_velocity: float32 [64, 120, 1024], P('gy', None, 'gx'), may hold values from -6 to 6
- meridional_edge_velocity: float32 [64, 120, 1024], P('gy', None, 'gx'), may hold values from -6 to 6
- scaled_warmth: float32 [64, 120, 1024], P('gy', None, 'gx'), may hold values from 0.5 to 2
- donor_depths: float32 [64, 120, 1024], P('gy', None, 'gx'), may hold values from 0.5 to 2
- leading_donor_level: int32 [64, 120, 1024], P('gy', None, 'gx'), may hold values from 0 to 118, as said below
- opening_share: bfloat16 [64, 120, 1024], P('gy', None, 'gx'), may hold values from 0 to 0.44921875
- closing_share: bfloat16 [64, 120, 1024], P('gy', None, 'gx'), may hold values from 0.546875 to 1
Outputs:
- tracers_out: float32 [8, 64, 120, 1024], P(None, 'gy', None, 'gx')
- regridded_zonal: float32 [64, 120, 1024], P('gy', None, 'gx')
- regridded_meridional: float32 [64, 120, 1024], P('gy', None, 'gx')
- adjusted_warmth: float32 [64, 120, 1024], P('gy', None, 'gx')
Inputs may be any that keep to these rules, and one draw needn't show every extreme that they name: Target layer k draws on source layers leading_donor_level and leading_donor_level + 1, and leading_donor_level lies within 2 of k.
All inputs are finite; a program needn't handle non-finite values.
Results may differ from a plain program's by a relative error of at most 0.0003.
Values sent between devices are 32-bit elements; how exact they have to be, the bound alone decides.
No kernel may reach another device: no remote copies, remote signals or barrier semaphores. Data moves between devices by JAX's collectives and lax.ppermute only.
A program may use at most 64 MiB of HBM per device.

v0:
```python
import jax
import jax.numpy as jnp
from jax import lax
from jax.sharding import Mesh
from jax.sharding import PartitionSpec as P

GY = ("gy_0", "gy_1", "gy_2")
GX = ("gx_0", "gx_1")
GX_GY = ("gx_0", "gx_1", "gy_0", "gy_1", "gy_2")


thermal_rescale_factor = 3.5
offsets_all = (-2, -1, 0, 1, 2, 3)


def passed_along(value, axis, steps):
    count = lax.axis_size(axis)
    pairs = [(source, (source + steps) % count) for source in range(count)]
    return lax.ppermute(value, axis, pairs)


def over_axes(x, axes):
    for axis in axes:
        x = lax.psum(x, axis)
    return x


def ppm_parts(values):
    layers = values.shape[-2]
    top_edge = 1.5 * values[..., 0:1, :] - 0.5 * values[..., 1:2, :]
    second_edge = 0.5 * (values[..., 0:1, :] + values[..., 1:2, :])
    inner_edge = 7.0 / 12.0 * (
        values[..., 1 : layers - 2, :] + values[..., 2 : layers - 1, :]
    ) - 1.0 / 12.0 * (values[..., 0 : layers - 3, :] + values[..., 3:layers, :])
    lower_edge = 0.5 * (
        values[..., layers - 2 : layers - 1, :] + values[..., layers - 1 : layers, :]
    )
    bottom_edge = (
        1.5 * values[..., layers - 1 : layers, :] - 0.5 * values[..., layers - 2 : layers - 1, :]
    )
    edge_values = jnp.concatenate(
        [top_edge, second_edge, inner_edge, lower_edge, bottom_edge], axis=-2
    )
    left_edge = edge_values[..., :layers, :]
    right_edge = edge_values[..., 1:, :]
    return (left_edge, right_edge - left_edge, 6.0 * values - 3.0 * (left_edge + right_edge))


def shifted_layers(values, amount):
    layers = values.shape[-2]
    if amount == 0:
        return values
    if amount > 0:
        filler = jnp.zeros(values.shape[:-2] + (amount, values.shape[-1]), values.dtype)
        return jnp.concatenate([values[..., amount:, :], filler], axis=-2)
    filler = jnp.zeros(values.shape[:-2] + (-amount, values.shape[-1]), values.dtype)
    return jnp.concatenate([filler, values[..., : layers + amount, :]], axis=-2)


def pick_layers(values, masks):
    total = jnp.zeros(values.shape, jnp.float32)
    for amount, selector in zip(offsets_all, masks):
        total = total + jnp.where(selector, shifted_layers(values, amount), 0.0)
    return total


def build_operator(donor_depths, leading_donor_level, opening_share, closing_share):
    start_frac = opening_share.astype(jnp.float32)
    end_frac = closing_share.astype(jnp.float32)
    layer_offset = leading_donor_level - lax.broadcasted_iota(
        jnp.int32, leading_donor_level.shape, 1
    )
    first_masks = [layer_offset == amount for amount in offsets_all]
    second_masks = [layer_offset + 1 == amount for amount in offsets_all]
    weight_first = (1.0 - start_frac) * pick_layers(donor_depths, first_masks)
    weight_second = end_frac * pick_layers(donor_depths, second_masks)
    linear_first = 0.5 * (start_frac + 1.0)
    square_first = linear_first - (start_frac * start_frac + start_frac + 1.0) / 3.0
    linear_second = 0.5 * end_frac
    square_second = linear_second - end_frac * end_frac / 3.0
    return (
        first_masks,
        second_masks,
        weight_first,
        weight_second,
        linear_first,
        square_first,
        linear_second,
        square_second,
    )


def multiply_by_regrid_operator(operator, values):
    (
        first_masks,
        second_masks,
        weight_first,
        weight_second,
        linear_first,
        square_first,
        linear_second,
        square_second,
    ) = operator
    left_edge, edge_slope, curvature = ppm_parts(values)
    mean_first = (
        pick_layers(left_edge, first_masks)
        + pick_layers(edge_slope, first_masks) * linear_first
        + pick_layers(curvature, first_masks) * square_first
    )
    mean_second = (
        pick_layers(left_edge, second_masks)
        + pick_layers(edge_slope, second_masks) * linear_second
        + pick_layers(curvature, second_masks) * square_second
    )
    return (weight_first * mean_first + weight_second * mean_second) / (
        weight_first + weight_second
    )


def local(
    species_means,
    zonal_edge_velocity,
    meridional_edge_velocity,
    scaled_warmth,
    donor_depths,
    leading_donor_level,
    opening_share,
    closing_share,
):
    vertical_regrid_operator = build_operator(
        donor_depths, leading_donor_level, opening_share, closing_share
    )
    regridded_depths = vertical_regrid_operator[2] + vertical_regrid_operator[3]
    mass_before = jnp.sum(species_means.astype(jnp.float32) * donor_depths, axis=(1, 2, 3))
    interior_u_faces = 0.5 * jnp.sum(
        0.5
        * (donor_depths[:-1] + donor_depths[1:])
        * zonal_edge_velocity[:-1]
        * zonal_edge_velocity[:-1]
    )
    interior_v_faces = 0.5 * jnp.sum(
        0.5
        * (donor_depths[:, :, :-1] + donor_depths[:, :, 1:])
        * meridional_edge_velocity[:, :, :-1]
        * meridional_edge_velocity[:, :, :-1]
    )
    local_prior_totals = (
        thermal_rescale_factor * jnp.sum(donor_depths * scaled_warmth)
        + interior_u_faces
        + interior_v_faces
    )
    from_south = passed_along(zonal_edge_velocity[-1:], GY, 1)
    u_paired = multiply_by_regrid_operator(
        vertical_regrid_operator,
        jnp.stack(
            [zonal_edge_velocity, jnp.concatenate([from_south, zonal_edge_velocity[:-1]], axis=0)]
        ),
    )
    u_cross = u_paired[1]
    returned = passed_along(
        jnp.stack([u_cross[0:1], donor_depths[0:1], regridded_depths[0:1]]), GY, -1
    )
    north_thick = returned[2]
    edge_u = 0.5 * jnp.sum(
        0.5
        * (donor_depths[-1:] + returned[1])
        * zonal_edge_velocity[-1:]
        * zonal_edge_velocity[-1:]
    )
    regridded_zonal = 0.5 * (u_paired[0] + jnp.concatenate([u_cross[1:], returned[0]], axis=0))
    zonal_following = 0.5 * jnp.sum(
        0.5
        * (regridded_depths + jnp.concatenate([regridded_depths[1:], north_thick], axis=0))
        * regridded_zonal
        * regridded_zonal
    )
    from_west = passed_along(meridional_edge_velocity[:, :, -1:], GX, 1)
    v_paired = multiply_by_regrid_operator(
        vertical_regrid_operator,
        jnp.stack(
            [
                meridional_edge_velocity,
                jnp.concatenate([from_west, meridional_edge_velocity[:, :, :-1]], axis=2),
            ]
        ),
    )
    v_cross = v_paired[1]
    v_returned = passed_along(
        jnp.stack([v_cross[:, :, 0:1], donor_depths[:, :, 0:1], regridded_depths[:, :, 0:1]]),
        GX,
        -1,
    )
    regridded_meridional = 0.5 * (
        v_paired[0] + jnp.concatenate([v_cross[:, :, 1:], v_returned[0]], axis=2)
    )
    edge_v = 0.5 * jnp.sum(
        0.5
        * (donor_depths[:, :, -1:] + v_returned[1])
        * meridional_edge_velocity[:, :, -1:]
        * meridional_edge_velocity[:, :, -1:]
    )
    meridional_following = 0.5 * jnp.sum(
        0.5
        * (regridded_depths + jnp.concatenate([regridded_depths[:, :, 1:], v_returned[2]], axis=2))
        * regridded_meridional
        * regridded_meridional
    )
    tracer_new = multiply_by_regrid_operator(
        vertical_regrid_operator, species_means.astype(jnp.float32)
    )
    regridded_warmth = multiply_by_regrid_operator(vertical_regrid_operator, scaled_warmth)
    mass_after = jnp.sum(tracer_new * regridded_depths, axis=(1, 2, 3))
    aggregate_regridded = jnp.sum(regridded_depths)
    kinetic_thermal_following = (
        thermal_rescale_factor * jnp.sum(regridded_depths * regridded_warmth)
        + zonal_following
        + meridional_following
    )
    mass_total_before, mass_total_after, scalars = (
        over_axes(mass_before, GX_GY),
        over_axes(mass_after, GX_GY),
        over_axes(
            jnp.stack(
                [
                    local_prior_totals + edge_u + edge_v,
                    kinetic_thermal_following,
                    aggregate_regridded,
                ]
            ),
            GX_GY,
        ),
    )
    enthalpy_global_preceding = scalars[0]
    enthalpy_global_following = scalars[1]
    thick_total = scalars[2]
    tracers_out = (
        tracer_new + ((mass_total_before - mass_total_after) / thick_total)[:, None, None, None]
    )
    adjusted_warmth = regridded_warmth + (enthalpy_global_preceding - enthalpy_global_following) / (
        thermal_rescale_factor * thick_total
    )
    return (tracers_out, regridded_zonal, regridded_meridional, adjusted_warmth)


def solution(mesh):
    split = Mesh(mesh.devices.reshape(4, 2, 8, 2, 2), ("gx_0", "gx_1", "gy_0", "gy_1", "gy_2"))
    in_specs = (
        P(None, GY, None, GX),
        P(GY, None, GX),
        P(GY, None, GX),
        P(GY, None, GX),
        P(GY, None, GX),
        P(GY, None, GX),
        P(GY, None, GX),
        P(GY, None, GX),
    )
    out_specs = (P(None, GY, None, GX), P(GY, None, GX), P(GY, None, GX), P(GY, None, GX))
    return jax.shard_map(local, mesh=split, in_specs=in_specs, out_specs=out_specs, check_vma=False)
```

profile of v0, /device:TPU:1, one launch (start us, length us, event | category | flops | bytes accessed | tf_op | source)
XLA Modules:
  0.0 101.0 jit_solution(2955615427944298031)
XLA Ops:
  0.6 1.7 %slice.551 = f32[2,120,1]{2,1,0:T(8,128)} slice(f32[2,120,128]{2,1,0:T(8,128)} %param.10), slice={[0:2], [0:120], [127:128]} | slice | bytes 1920 | tf_op jit(solution)/shard_map/slice | solution.py:177
  2.3 3.6 %collective-permute-start.2 = (f32[2,120,1]{2,1,0:T(8,128)}, f32[2,120,1]{2,1,0:T(8,128)S(1)}, u32[]{:S(2)}, u32[]{:S(2)}) collective-permute-start(f32[2,120,1]{2,1,0:T(8,128)} %slice.551), channel_id=1, source_target_pairs={{0,32},{32,64},{64,96},{96,128},{128,160},{160,192},{192,224},{224... | collective-permute-start | bytes 2888 | tf_op jit(solution)/shard_map/ppermute | solution.py:19
  5.9 0.6 fusion.103
  6.5 1.2 %collective-permute-start = (f32[1,120,128]{2,1,0:T(8,128)}, f32[1,120,128]{2,1,0:T(8,128)}, u32[]{:S(2)}, u32[]{:S(2)}) collective-permute-start(f32[1,120,128]{2,1,0:T(8,128)} %get-tuple-element.129), channel_id=1, source_target_pairs={{0,1},{1,2},{2,3},{3,4},{4,5},{5,6},{6,7},{7,8},{8,9},{9,10},{10,1... | collective-permute-start | bytes 184328 | tf_op jit(solution)/shard_map/ppermute | solution.py:19
  7.8 1.0 copy-done.2
  8.8 0.4 fusion.5
  9.2 0.6 fusion.7
  9.8 0.1 slice.631
  9.8 0.4 fusion.86
  10.2 0.4 fusion.87
  10.6 0.1 slice.626
  10.6 0.1 fusion
  10.7 0.1 pad_maximum_fusion.2
  10.8 0.1 pad_maximum_fusion.3
  10.9 0.8 copy-done.1
  11.7 0.7 fusion.46
  12.4 0.1 copy-done.12
  12.6 0.1 copy-done.15
  12.7 0.4 fusion.51
  13.1 0.1 slice_reduce_fusion
  13.2 0.7 fusion.102
  13.9 0.3 copy-done.3
  14.3 0.7 fusion.61
  15.0 0.8 fusion.98
  15.7 0.8 fusion.99
  16.5 0.7 fusion.40
  17.2 0.7 pad_maximum_fusion.20
  17.9 7.7 %multiply_reduce_fusion = (f32[8]{0:T(128)S(1)}, f32[8,2,120,128]{3,2,1,0:T(8,128)S(1)}) fusion(f32[2,120,128]{2,1,0:T(8,128)S(1)} %get-tuple-element.137, f32[2,120,128]{2,1,0:T(8,128)S(1)} %get-tuple-element.153, f32[2,120,128]{2,1,0:T(8,128)S(1)} %get-tuple-element.152, pred[2,120,128]{2,1,0:T(8,128)(4,1)S(1)} %get-tuple-element.139, ...), kind=kLoop, calls=%fused_computation.18 | loop fusion | flops 24084472 | bytes 17244192 | tf_op jit(solution)/shard_map/reduce_sum | solution.py:212
  25.6 0.8 slice.715
  26.4 0.7 slice.709
  27.1 0.7 slice.704
  29.0 0.1 maximum_bitcast_fusion.1
  29.2 0.1 fusion.19
  29.3 0.1 fusion.38
  29.7 1.0 add_divide_fusion.1
  30.7 0.1 slice_reduce_fusion.1
  30.8 0.8 slice.718
  31.6 3.8 %collective-permute-start.3 = (f32[3,2,120,1]{2,1,3,0:T(2,128)S(1)}, f32[3,2,120,1]{2,1,3,0:T(2,128)S(1)}, u32[]{:S(2)}, u32[]{:S(2)}) collective-permute-start(f32[3,2,120,1]{2,1,3,0:T(2,128)S(1)} %pad_maximum_fusion.23), channel_id=1, source_target_pairs={{0,224},{32,0},{64,32},{96,64},{128,96},{160,128},{192,160},{224,1... | collective-permute-start | bytes 8648 | tf_op jit(solution)/shard_map/ppermute | solution.py:19
  35.4 0.8 maximum_bitcast_fusion
  36.3 0.1 fusion.30
  36.4 0.1 fusion.39
  36.8 1.0 add_divide_fusion.2
  37.8 0.6 slice_bitcast_fusion.4
  38.5 0.2 copy-done.11
  38.7 0.7 pad_maximum_fusion.17
  39.4 0.3 collective-permute-start.1
  39.6 0.8 copy.187
  40.4 0.8 copy.188
  41.2 0.1 copy.180
  41.4 0.7 fusion.47
  42.7 2.0 %collective-permute-done.1 = f32[3,1,120,128]{3,2,1,0:T(8,128)} collective-permute-done((f32[3,1,120,128]{3,2,1,0:T(8,128)}, f32[3,1,120,128]{3,2,1,0:T(8,128)}, u32[]{:S(2)}, u32[]{:S(2)}) %collective-permute-start.1) | collective-permute-done | bytes 184352 | tf_op jit(solution)/shard_map/ppermute | solution.py:19
  44.6 0.9 slice_bitcast_fusion.3
  45.6 3.6 %fusion.49 = (f32[]{:T(128)}, f32[]{:T(128)}, f32[]{:T(128)}, f32[]{:T(128)}, f32[2,120,128]{2,1,0:T(8,128)}, /*index=5*/f32[2,120,128]{2,1,0:T(8,128)}, f32[2,120,128]{2,1,0:T(8,128)}) fusion(f32[2,120,128]{2,1,0:T(8,128)S(1)} %get-tuple-element.137, f32[2,120,1]{2,1,0:T(8,128)} %copy.187, f32[2,120,127]{2,1,0:T(8,128)} %slice.715, ...), kind=kLoop, calls=%fused_computation.136 | loop fusion | flops 3839996 | bytes 3906576 | tf_op jit(solution)/shard_map/reduce_sum | solution.py:202
  51.1 1.5 %fusion.63 = (f32[]{:T(128)}, f32[]{:T(128)}) fusion(f32[3,1,120,128]{3,2,1,0:T(8,128)} %collective-permute-done.1, f32[2,120,128]{2,1,0:T(8,128)S(1)} %copy-done, f32[2,120,128]{2,1,0:T(8,128)S(1)} %copy-done.4), kind=kLoop, calls=%fused_computation.176 | loop fusion | flops 153598 | bytes 307208 | tf_op jit(solution)/shard_map/reduce_sum | solution.py:164
  53.9 0.7 pad_maximum_fusion.24
  54.6 7.5 %all-reduce.66 = (f32[8]{0:T(128)S(1)}, f32[8]{0:T(128)S(1)}, f32[3]{0:T(128)S(1)}) all-reduce(f32[8]{0:T(128)S(1)} %get-tuple-element.79, f32[8]{0:T(128)S(1)} %get-tuple-element.48, f32[3]{0:T(128)S(1)} %pad_maximum_fusion.24), channel_id=1, replica_groups=mesh['gx_0'=4,'gx_1'=2,'gy_0'=8,'gy_1'=2,'gy_2'=2] {'gx_0'}, use_global_device_ids=true, to_apply=%region_1.2 | all-reduce | flops 19 | bytes 152 | tf_op jit(solution)/shard_map/psum | solution.py:24
  62.1 5.3 %all-reduce.69 = (f32[8]{0:T(128)S(1)}, f32[8]{0:T(128)S(1)}, f32[3]{0:T(128)S(1)}) all-reduce(f32[8]{0:T(128)S(1)} %get-tuple-element.21, f32[8]{0:T(128)S(1)} %get-tuple-element.22, f32[3]{0:T(128)S(1)} %get-tuple-element.23), channel_id=1, replica_groups=mesh['gx_0'=4,'gx_1'=2,'gy_0'=8,'gy_1'=2,'gy_2'=2] {'gx_1'}, use_global_device_ids=true, to_apply=%region_2.3 | all-reduce | flops 19 | bytes 152 | tf_op jit(solution)/shard_map/psum | solution.py:24
  67.3 16.3 %all-reduce.65 = (f32[8]{0:T(128)S(1)}, f32[8]{0:T(128)S(1)}, f32[3]{0:T(128)S(1)}) all-reduce(f32[8]{0:T(128)S(1)} %get-tuple-element.30, f32[8]{0:T(128)S(1)} %get-tuple-element.31, f32[3]{0:T(128)S(1)} %get-tuple-element.32), channel_id=1, replica_groups=mesh['gx_0'=4,'gx_1'=2,'gy_0'=8,'gy_1'=2,'gy_2'=2] {'gy_0'}, use_global_device_ids=true, to_apply=%region_3.4 | all-reduce | flops 19 | bytes 152 | tf_op jit(solution)/shard_map/psum | solution.py:24
  83.6 3.8 %all-reduce.68 = (f32[8]{0:T(128)S(1)}, f32[8]{0:T(128)S(1)}, f32[3]{0:T(128)S(1)}) all-reduce(f32[8]{0:T(128)S(1)} %get-tuple-element.18, f32[8]{0:T(128)S(1)} %get-tuple-element.19, f32[3]{0:T(128)S(1)} %get-tuple-element.20), channel_id=1, replica_groups=mesh['gx_0'=4,'gx_1'=2,'gy_0'=8,'gy_1'=2,'gy_2'=2] {'gy_1'}, use_global_device_ids=true, to_apply=%region_4.5 | all-reduce | flops 19 | bytes 152 | tf_op jit(solution)/shard_map/psum | solution.py:24
  87.4 8.6 %all-reduce.67 = (f32[8]{0:T(128)S(1)}, f32[8]{0:T(128)S(1)}, f32[3]{0:T(128)S(1)}) all-reduce(f32[8]{0:T(128)S(1)} %get-tuple-element.27, f32[8]{0:T(128)S(1)} %get-tuple-element.28, f32[3]{0:T(128)S(1)} %get-tuple-element.29), channel_id=1, replica_groups=mesh['gx_0'=4,'gx_1'=2,'gy_0'=8,'gy_1'=2,'gy_2'=2] {'gy_2'}, use_global_device_ids=true, to_apply=%region_5.6 | all-reduce | flops 19 | bytes 152 | tf_op jit(solution)/shard_map/psum | solution.py:24
  95.9 0.6 fusion.106
  97.2 0.7 subtract_divide_fusion
  97.9 1.1 %broadcast_add_fusion = f32[8,2,120,128]{3,2,1,0:T(8,128)} fusion(f32[8,2,120,128]{3,2,1,0:T(8,128)S(1)} %get-tuple-element.49, f32[8]{0:T(128)S(1)} %subtract_divide_fusion), kind=kLoop, calls=%fused_computation.57 | loop fusion | flops 245760 | bytes 1966112 | tf_op jit(solution)/shard_map/add | solution.py:237
  100.3 0.7 broadcast_add_fusion.1
  (66 shorter events, 1.0 us)
Async XLA Ops:
  0.6 5.3 %copy-start.4 = (f32[2,120,128]{2,1,0:T(8,128)S(1)}, f32[2,120,128]{2,1,0:T(8,128)}, u32[]{:S(2)}) copy-start(f32[2,120,128]{2,1,0:T(8,128)} %param.9) | copy-start | bytes 368644
  2.3 5.4 %copy-start = (f32[2,120,128]{2,1,0:T(8,128)S(1)}, f32[2,120,128]{2,1,0:T(8,128)}, u32[]{:S(2)}) copy-start(f32[2,120,128]{2,1,0:T(8,128)} %param.12) | copy-start | bytes 368644
  2.3 26.7 %collective-permute-start.2 = (f32[2,120,1]{2,1,0:T(8,128)}, f32[2,120,1]{2,1,0:T(8,128)S(1)}, u32[]{:S(2)}, u32[]{:S(2)}) collective-permute-start(f32[2,120,1]{2,1,0:T(8,128)} %slice.551), channel_id=1, source_target_pairs={{0,32},{32,64},{64,96},{96,128},{128,160},{160,192},{192,224},{224... | collective-permute-start | bytes 2888 | tf_op jit(solution)/shard_map/ppermute | solution.py:19
  6.5 28.9 %collective-permute-start = (f32[1,120,128]{2,1,0:T(8,128)}, f32[1,120,128]{2,1,0:T(8,128)}, u32[]{:S(2)}, u32[]{:S(2)}) collective-permute-start(f32[1,120,128]{2,1,0:T(8,128)} %get-tuple-element.129), channel_id=1, source_target_pairs={{0,1},{1,2},{2,3},{3,4},{4,5},{5,6},{6,7},{7,8},{8,9},{9,10},{10,1... | collective-permute-start | bytes 184328 | tf_op jit(solution)/shard_map/ppermute | solution.py:19
  7.7 1.0 %copy-start.2 = (bf16[8,2,120,128]{3,2,1,0:T(8,128)(2,1)S(1)}, bf16[8,2,120,128]{3,2,1,0:T(8,128)(2,1)}, u32[]{:S(2)}) copy-start(bf16[8,2,120,128]{3,2,1,0:T(8,128)(2,1)} %param.8) | copy-start | bytes 1474564
  10.8 0.9 copy-start.1
  11.7 0.8 copy-start.12
  11.7 0.9 copy-start.13
  11.7 1.0 copy-start.15
  13.2 1.0 copy-start.3
  31.6 8.0 %collective-permute-start.3 = (f32[3,2,120,1]{2,1,3,0:T(2,128)S(1)}, f32[3,2,120,1]{2,1,3,0:T(2,128)S(1)}, u32[]{:S(2)}, u32[]{:S(2)}) collective-permute-start(f32[3,2,120,1]{2,1,3,0:T(2,128)S(1)} %pad_maximum_fusion.23), channel_id=1, source_target_pairs={{0,224},{32,0},{64,32},{96,64},{128,96},{160,128},{192,160},{224,1... | collective-permute-start | bytes 8648 | tf_op jit(solution)/shard_map/ppermute | solution.py:19
  37.8 0.8 copy-start.11
  39.4 5.3 %collective-permute-start.1 = (f32[3,1,120,128]{3,2,1,0:T(8,128)}, f32[3,1,120,128]{3,2,1,0:T(8,128)}, u32[]{:S(2)}, u32[]{:S(2)}) collective-permute-start(f32[3,1,120,128]{3,2,1,0:T(8,128)} %pad_maximum_fusion.17), channel_id=1, source_target_pairs={{0,31},{1,0},{2,1},{3,2},{4,3},{5,4},{6,5},{7,6},{8,7},{9,8},{10,9... | collective-permute-start | bytes 552968 | tf_op jit(solution)/shard_map/ppermute | solution.py:19
  40.4 5.1 %copy-start.7 = (f32[2,118,128]{2,1,0:T(8,128)S(1)}, f32[2,118,128]{2,1,0:T(8,128)}, u32[]{:S(2)}) copy-start(f32[2,118,128]{2,1,0:T(8,128)} %get-tuple-element.168) | copy-start | bytes 362500
  40.4 5.1 %copy-start.8 = (f32[2,118,128]{2,1,0:T(8,128)S(1)}, f32[2,118,128]{2,1,0:T(8,128)}, u32[]{:S(2)}) copy-start(f32[2,118,128]{2,1,0:T(8,128)} %get-tuple-element.169) | copy-start | bytes 362500
  40.4 5.1 %copy-start.14 = (f32[1,120,128]{2,1,0:T(8,128)S(1)}, f32[1,120,128]{2,1,0:T(8,128)}, u32[]{:S(2)}) copy-start(f32[1,120,128]{2,1,0:T(8,128)} %get-tuple-element.127) | copy-start | bytes 184324
  41.2 4.3 %copy-start.9 = (f32[2,119,128]{2,1,0:T(8,128)S(1)}, f32[2,119,128]{2,1,0:T(8,128)}, u32[]{:S(2)}) copy-start(f32[2,119,128]{2,1,0:T(8,128)} %get-tuple-element.121) | copy-start | bytes 365572
  42.6 2.9 %copy-start.5 = (f32[2,118,128]{2,1,0:T(8,128)S(1)}, f32[2,118,128]{2,1,0:T(8,128)}, u32[]{:S(2)}) copy-start(f32[2,118,128]{2,1,0:T(8,128)} %get-tuple-element.119) | copy-start | bytes 362500
  42.7 2.9 %copy-start.6 = (f32[2,118,128]{2,1,0:T(8,128)S(1)}, f32[2,118,128]{2,1,0:T(8,128)}, u32[]{:S(2)}) copy-start(f32[2,118,128]{2,1,0:T(8,128)} %get-tuple-element.120) | copy-start | bytes 362500
  97.8 2.5 %copy-start.10 = (f32[2,120,128]{2,1,0:T(8,128)S(1)}, f32[2,120,128]{2,1,0:T(8,128)}, u32[]{:S(2)}) copy-start(f32[2,120,128]{2,1,0:T(8,128)} %get-tuple-element.33) | copy-start | bytes 368644
where the time goes:
time: 102 us; the launch traced here: 101 us
  blocking collectives  41.4 us (41%)
  other arithmetic  25.3 us (25%)
  local copies, waits for them, and re-layouts  15.3 us (15%)
  starting transfers between devices  8.84 us (9%)
  between operations  8.16 us (8%)
  waiting for transfers between devices  1.97 us (2%)
    psum x5, blocking collectives, over_axes(): x = lax.psum(x, axis)  41.4 us
    ppermute x4, starting transfers between devices, passed_along(): return lax.ppermute(value, axis, pairs)  8.84 us
    reduce_sum x1, other arithmetic, local(): mass_after = jnp.sum(tracer_new * regridded_depths, axis=(1, 2, 3))  7.73 us
    reduce_sum x1, other arithmetic, local(): jnp.sum(0.5 * (regridded_depths + jnp.concatenate([regridded_depths[:, :,...  3.63 us
    unnamed x33, local copies, waits for them, and re-layouts  2.61 us
    slice x14, local copies, waits for them, and re-layouts, shifted_layers(): return jnp.concatenate([filler, values[..., :layers + amount, :]], axis=-2)  2.61 us
  transfers between devices with their start and end apart: 4, of which 1 were waited for; matrix products, arithmetic and copies ran while one was open for 26% of the time, Pallas kernels for 0%

commit v1 on v0

v1 whole, which is shorter than its diff:
```python
import functools

import jax
import jax.numpy as jnp
from jax import lax
from jax.experimental import pallas as pl
from jax.experimental.pallas import tpu as pltpu
from jax.sharding import PartitionSpec as P

HEAT = 3.5
PAD = 8
STEP = 8
DIAGONALS = tuple(range(-4, 6))
C7 = 7.0 / 12.0
C1 = 1.0 / 12.0


def block_of(k):
    return pl.ds(pl.multiple_of(k * STEP, STEP), STEP)


def padded_block(k):
    return pl.ds(pl.multiple_of(k * STEP + PAD, STEP), STEP)


def shifted(ref, k, *lead):
    return lambda d: ref[(*lead, pl.ds(k * STEP + (PAD + d), STEP), slice(None))]


def clear_pads(ref, layers):
    lead = ref.shape[:-2]
    zero = jnp.zeros(lead + (PAD, ref.shape[-1]), ref.dtype)
    every = (slice(None),) * len(lead)
    ref[(*every, pl.ds(0, PAD), slice(None))] = zero
    ref[(*every, pl.ds(PAD + layers, PAD), slice(None))] = zero


def pick(masks, values):
    chosen = values[-1]
    for mask, value in zip(masks[-2::-1], values[-2::-1]):
        chosen = jnp.where(mask, value, chosen)
    return chosen


def operator(depth, level, start, end, k, layers):
    offset = level - (lax.broadcasted_iota(jnp.int32, level.shape, 0) + k * STEP)
    masks = [offset == o for o in (-2, -1, 0, 1, 2)]
    depths = [depth(d) for d in range(-2, 4)]
    weight_first = (1.0 - start) * pick(masks, depths[0:5])
    weight_second = end * pick(masks, depths[1:6])
    thick = weight_first + weight_second
    inverse = 1.0 / thick
    first = weight_first * inverse
    second = weight_second * inverse
    linear_first = 0.5 * (start + 1.0)
    square_first = linear_first - (start * start + start + 1.0) * (1.0 / 3.0)
    linear_second = 0.5 * end
    square_second = linear_second - end * end * (1.0 / 3.0)
    triple_first = 3.0 * square_first
    triple_second = 3.0 * square_second
    edge0 = first * (1.0 - linear_first - triple_first)
    edge1 = first * (linear_first - triple_first) + second * (
        1.0 - linear_second - triple_second
    )
    edge2 = second * (linear_second - triple_second)
    mean0 = first * (2.0 * triple_first)
    mean1 = second * (2.0 * triple_second)
    top, under_top = level == 0, level == 1
    bottom, over_bottom = level == layers - 2, level == layers - 3
    e0 = (
        jnp.where(top | under_top, 0.0, -C1),
        jnp.where(top, 0.0, jnp.where(under_top, 0.5, C7)),
        jnp.where(top, 1.5, jnp.where(under_top, 0.5, C7)),
        jnp.where(top, -0.5, jnp.where(under_top, 0.0, -C1)),
    )
    outer = jnp.where(top | bottom, 0.0, -C1)
    inner = jnp.where(top | bottom, 0.5, C7)
    e2 = (
        jnp.where(bottom, -0.5, jnp.where(over_bottom, 0.0, -C1)),
        jnp.where(bottom, 1.5, jnp.where(over_bottom, 0.5, C7)),
        jnp.where(bottom, 0.0, jnp.where(over_bottom, 0.5, C7)),
        jnp.where(bottom | over_bottom, 0.0, -C1),
    )
    taps = {
        -2: e0[0] * edge0,
        -1: e0[1] * edge0 + outer * edge1,
        0: e0[2] * edge0 + inner * edge1 + e2[0] * edge2 + mean0,
        1: e0[3] * edge0 + inner * edge1 + e2[1] * edge2 + mean1,
        2: outer * edge1 + e2[2] * edge2,
        3: e2[3] * edge2,
    }
    diagonals = []
    for d in DIAGONALS:
        value = jnp.zeros_like(thick)
        for mask, o in zip(masks, (-2, -1, 0, 1, 2)):
            if d - o in taps:
                value = jnp.where(mask, taps[d - o], value)
        diagonals.append(value)
    return thick, diagonals


def apply_operator(diagonals, values):
    total = None
    for d, weight in zip(DIAGONALS, diagonals):
        term = weight * values(d)
        total = term if total is None else total + term
    return total


def pack_body(depth_ref, level_ref, start_ref, end_ref, row_ref, column_ref):
    layers = depth_ref.shape[1]
    rows = depth_ref.shape[0]

    def step(k, carry):
        block = block_of(k)
        lane = lax.broadcasted_iota(jnp.int32, (STEP, 128), 1)
        packed = jnp.zeros((STEP, 128), jnp.float32)
        for i, ref in enumerate((depth_ref, level_ref, start_ref, end_ref)):
            for r in range(rows):
                value = ref[r, block, :].astype(jnp.float32)
                if r == 0:
                    row_ref[i, block, :] = value
                target = i * rows + r
                if target:
                    value = pltpu.roll(value, target, 1)
                packed = jnp.where(lane == target, value, packed)
        column_ref[block, :] = packed
        return carry

    lax.fori_loop(0, layers // STEP, step, 0)


def sums_body(
    species_ref,
    zonal_ref,
    merid_ref,
    warmth_ref,
    depth_ref,
    level_ref,
    start_ref,
    end_ref,
    row_ref,
    column_ref,
    zonal_out,
    merid_out,
    sums_out,
    depth_pad,
    zonal_pad,
    merid_pad,
    west_pad,
    last_pad,
    adjoint_pad,
    thick_s,
    across_s,
    cross_s,
):
    tracers = species_ref.shape[0]
    rows, layers, _ = depth_ref.shape
    blocks = layers // STEP
    north, east = rows, rows + 1
    for ref in (depth_pad, zonal_pad, merid_pad, west_pad, last_pad, adjoint_pad):
        clear_pads(ref, layers)
    lane = lax.broadcasted_iota(jnp.int32, (STEP, 128), 1)

    def spread(k, carry):
        block, target = block_of(k), padded_block(k)
        last = jnp.zeros((STEP, 128), jnp.float32)
        for r in range(rows):
            depth_pad[r, target, :] = depth_ref[r, block, :]
            zonal_pad[r, target, :] = zonal_ref[r, block, :]
            value = merid_ref[r, block, :]
            merid_pad[r, target, :] = value
            west_pad[r, target, :] = pltpu.roll(value, 1, 1)
            last = jnp.where(lane == r, pltpu.roll(value, r + 1, 1), last)
        last_pad[target, :] = last
        depth_pad[north, target, :] = row_ref[0, block, :]
        depth_pad[east, target, :] = column_ref[block, :]
        return carry

    lax.fori_loop(0, blocks, spread, 0)

    def halo(k, carry):
        block = block_of(k)
        thick, diagonals = operator(
            shifted(depth_pad, k, north),
            row_ref[1, block, :].astype(jnp.int32),
            row_ref[2, block, :],
            row_ref[3, block, :],
            k,
            layers,
        )
        thick_s[north, block, :] = thick
        cross_s[rows - 1, block, :] = apply_operator(
            diagonals, shifted(zonal_pad, k, rows - 1)
        )
        packed = column_ref[block, :]
        thick, diagonals = operator(
            shifted(depth_pad, k, east),
            pltpu.roll(packed, 128 - rows, 1).astype(jnp.int32),
            pltpu.roll(packed, 128 - 2 * rows, 1),
            pltpu.roll(packed, 128 - 3 * rows, 1),
            k,
            layers,
        )
        thick_s[east, block, :] = thick
        across_s[rows, block, :] = apply_operator(diagonals, shifted(last_pad, k))
        return carry

    lax.fori_loop(0, blocks, halo, 0)

    def own(k, carry):
        block, target = block_of(k), padded_block(k)
        for r in range(rows):
            thick, diagonals = operator(
                shifted(depth_pad, k, r),
                level_ref[r, block, :],
                start_ref[r, block, :].astype(jnp.float32),
                end_ref[r, block, :].astype(jnp.float32),
                k,
                layers,
            )
            thick_s[r, block, :] = thick
            zonal_out[r, block, :] = apply_operator(diagonals, shifted(zonal_pad, k, r))
            merid_out[r, block, :] = apply_operator(diagonals, shifted(merid_pad, k, r))
            across_s[r, block, :] = apply_operator(diagonals, shifted(west_pad, k, r))
            if r:
                cross_s[r - 1, block, :] = apply_operator(
                    diagonals, shifted(zonal_pad, k, r - 1)
                )
            for i, weight in enumerate(diagonals):
                adjoint_pad[r, i, target, :] = thick * weight
        return carry

    lax.fori_loop(0, blocks, own, 0)

    def totals(k, carry):
        block = block_of(k)
        masses, energy, total = list(carry[:-2]), carry[-2], carry[-1]
        for r in range(rows):
            depth = depth_ref[r, block, :]
            back = None
            for i, d in enumerate(DIAGONALS):
                term = adjoint_pad[r, i, pl.ds(k * STEP + (PAD - d), STEP), :]
                back = term if back is None else back + term
            lost = depth - back
            for t in range(tracers):
                masses[t] = masses[t] + species_ref[t, r, block, :].astype(jnp.float32) * lost
            energy = energy + HEAT * (warmth_ref[r, block, :] * lost)
            thick = thick_s[r, block, :]
            total = total + thick
            zonal = 0.5 * (zonal_out[r, block, :] + cross_s[r, block, :])
            zonal_out[r, block, :] = zonal
            wind = zonal_ref[r, block, :]
            depth_next = depth_ref[r + 1, block, :] if r + 1 < rows else row_ref[0, block, :]
            thick_next = thick_s[r + 1, block, :]
            energy = energy + 0.25 * (
                (depth + depth_next) * (wind * wind) - (thick + thick_next) * (zonal * zonal)
            )

            def eastward(own_value, edge_value):
                return jnp.where(
                    lane == 127,
                    pltpu.roll(edge_value, 127 - r, 1),
                    pltpu.roll(own_value, 127, 1),
                )

            merid = 0.5 * (
                merid_out[r, block, :]
                + eastward(across_s[r, block, :], across_s[rows, block, :])
            )
            merid_out[r, block, :] = merid
            wind = merid_ref[r, block, :]
            depth_next = eastward(depth, column_ref[block, :])
            thick_next = eastward(thick, thick_s[east, block, :])
            energy = energy + 0.25 * (
                (depth + depth_next) * (wind * wind) - (thick + thick_next) * (merid * merid)
            )
        return (*masses, energy, total)

    zero = jnp.zeros((STEP, 128), jnp.float32)
    parts = lax.fori_loop(0, blocks, totals, (zero,) * (tracers + 2))
    row = jnp.zeros((STEP, 128), jnp.float32)
    for i, part in enumerate(parts):
        row = jnp.where(lane == i, jnp.sum(part, axis=1, keepdims=True), row)
    row = jnp.sum(row, axis=0, keepdims=True)
    sums_out[...] = jnp.broadcast_to(row, sums_out.shape)


def remap_body(
    species_ref,
    warmth_ref,
    depth_ref,
    level_ref,
    start_ref,
    end_ref,
    tracers_out,
    warmth_out,
    depth_pad,
    field_pad,
):
    tracers = species_ref.shape[0]
    rows, layers, _ = depth_ref.shape
    blocks = layers // STEP
    clear_pads(depth_pad, layers)
    clear_pads(field_pad, layers)

    def spread(k, carry):
        block, target = block_of(k), padded_block(k)
        for r in range(rows):
            depth_pad[r, target, :] = depth_ref[r, block, :]
            field_pad[tracers, r, target, :] = warmth_ref[r, block, :]
            for t in range(tracers):
                field_pad[t, r, target, :] = species_ref[t, r, block, :].astype(jnp.float32)
        return carry

    lax.fori_loop(0, blocks, spread, 0)

    def own(k, carry):
        block = block_of(k)
        for r in range(rows):
            _, diagonals = operator(
                shifted(depth_pad, k, r),
                level_ref[r, block, :],
                start_ref[r, block, :].astype(jnp.float32),
                end_ref[r, block, :].astype(jnp.float32),
                k,
                layers,
            )
            for t in range(tracers):
                tracers_out[t, r, block, :] = apply_operator(
                    diagonals, shifted(field_pad, k, t, r)
                )
            warmth_out[r, block, :] = apply_operator(
                diagonals, shifted(field_pad, k, tracers, r)
            )
        return carry

    lax.fori_loop(0, blocks, own, 0)


def ring_shift(value, axis, steps):
    count = lax.axis_size(axis)
    return lax.ppermute(value, axis, [(i, (i + steps) % count) for i in range(count)])


def cost(flops, moved):
    return pl.CostEstimate(flops=flops, bytes_accessed=moved, transcendentals=0)


def local(
    species,
    zonal,
    merid,
    warmth,
    depth,
    level,
    start,
    end,
):
    tracers = species.shape[0]
    rows, layers, columns = depth.shape
    devices = lax.axis_size(("gx", "gy"))
    f32 = functools.partial(jax.ShapeDtypeStruct, dtype=jnp.float32)
    vmem = pl.BlockSpec(memory_space=pltpu.VMEM)
    plane = (rows, layers, columns)
    tall = layers + 2 * PAD
    row_halo, column_halo = pl.pallas_call(
        pack_body,
        out_shape=(f32((4, layers, columns)), f32((layers, columns))),
        in_specs=[vmem] * 4,
        out_specs=(vmem, vmem),
        cost_estimate=cost(100_000, 600_000),
        name="pack_halo",
    )(depth, level, start, end)
    column_halo = ring_shift(column_halo, "gx", -1)
    row_halo = ring_shift(row_halo, "gy", -1)
    zonal_new, merid_new, sums = pl.pallas_call(
        sums_body,
        out_shape=(f32(plane), f32(plane), f32((devices, 128))),
        in_specs=[vmem] * 10,
        out_specs=(vmem,) * 3,
        scratch_shapes=[
            pltpu.VMEM((rows + 2, tall, columns), jnp.float32),
            pltpu.VMEM((rows, tall, columns), jnp.float32),
            pltpu.VMEM((rows, tall, columns), jnp.float32),
            pltpu.VMEM((rows, tall, columns), jnp.float32),
            pltpu.VMEM((tall, columns), jnp.float32),
            pltpu.VMEM((rows, len(DIAGONALS), tall, columns), jnp.float32),
            pltpu.VMEM((rows + 2, layers, columns), jnp.float32),
            pltpu.VMEM((rows + 1, layers, columns), jnp.float32),
            pltpu.VMEM((rows, layers, columns), jnp.float32),
        ],
        cost_estimate=cost(20_000_000, 2_000_000),
        name="wind_and_sums",
    )(species, zonal, merid, warmth, depth, level, start, end, row_halo, column_halo)
    gathered = lax.all_to_all(
        sums.reshape(devices, 1, 128), ("gx", "gy"), 0, 0, tiled=True
    )
    tracer_new, warmth_new = pl.pallas_call(
        remap_body,
        out_shape=(f32((tracers, *plane)), f32(plane)),
        in_specs=[vmem] * 6,
        out_specs=(vmem,) * 2,
        scratch_shapes=[
            pltpu.VMEM((rows, tall, columns), jnp.float32),
            pltpu.VMEM((tracers + 1, rows, tall, columns), jnp.float32),
        ],
        cost_estimate=cost(20_000_000, 2_000_000),
        name="tracer_remap",
    )(species, warmth, depth, level, start, end)
    totals = jnp.sum(gathered, axis=(0, 1))
    total = totals[tracers + 1]
    tracers_out = tracer_new + (totals[:tracers] / total)[:, None, None, None]
    warmth_out = warmth_new + totals[tracers] / (HEAT * total)
    return tracers_out, zonal_new, merid_new, warmth_out


def solution(mesh):
    plane = P("gy", None, "gx")
    stack = P(None, "gy", None, "gx")
    return jax.shard_map(
        local,
        mesh=mesh,
        in_specs=(stack,) + (plane,) * 7,
        out_specs=(stack, plane, plane, plane),
        check_vma=False,
    )
```

time: 102 us -> 55.1 us (0.54)
  blocking collectives: 41.4 us -> 0 us
  other arithmetic: 25.3 us -> 3.85 us
  Pallas kernels: 0 us -> 13.5 us
  local copies, waits for them, and re-layouts: 15.3 us -> 1.97 us
  starting transfers between devices: 8.84 us -> 20.7 us
  waiting for transfers between devices: 1.97 us -> 12.9 us
  between operations: 8.16 us -> 1.98 us
    psum x5 -> x0, blocking collectives: 41.4 us -> none  [over_axes(): x = lax.psum(x, axis)]
    all_to_all x0 -> x1, starting transfers between devices: none -> 14 us  [local(): lax.all_to_all(sums.reshape(devices, 1, 128), ('gx', 'gy'), 0, 0, tiled=T...]
    reduce_sum x5 -> x1, other arithmetic: 14.3 us -> 0.29 us  [local(): totals = jnp.sum(gathered, axis=(0, 1))]
    pallas_call x0 -> x3, Pallas kernels: none -> 13.5 us  [the longest x1 7.03 us: local(): pl.pallas_call(sums_body, out_shape=(f32(plane), f32(plane), f32((devices...]
    slice x32 -> x1, local copies, waits for them, and re-layouts: 10.1 us -> 0.65 us  [local(): warmth_out = warmth_new + totals[tracers] / (HEAT * total)]
    all_to_all x0 -> x1, waiting for transfers between devices: none -> 9.18 us  [local(): lax.all_to_all(sums.reshape(devices, 1, 128), ('gx', 'gy'), 0, 0, tiled=T...]
    squeeze x6 -> x0, local copies, waits for them, and re-layouts: 2.59 us -> none  [the longest x1 0.87 us: local(): returned[0]]
    another operation x5 -> x0, other arithmetic: 2.34 us -> none  [the longest x1 0.84 us: local(): jnp.stack([zonal_edge_velocity, jnp.concatenate([from_south, zonal_edge_v...]
  transfers between devices with their start and end apart: 4 -> 3, of which waited for: 1 -> 2; matrix products, arithmetic and copies ran while one was open for 26% -> 0% of each run, Pallas kernels for 0% -> 7%
where the time goes in v1:
time: 55.1 us; the launch traced here: 54.9 us
  starting transfers between devices  20.7 us (38%)
  Pallas kernels  13.5 us (25%)
  waiting for transfers between devices  12.9 us (23%)
  other arithmetic  3.85 us (7%)
  between operations  1.98 us (4%)
  local copies, waits for them, and re-layouts  1.97 us (4%)
    all_to_all x1, starting transfers between devices, local(): lax.all_to_all(sums.reshape(devices, 1, 128), ('gx', 'gy'), 0, 0, tiled=T...  14 us
    all_to_all x1, waiting for transfers between devices, local(): lax.all_to_all(sums.reshape(devices, 1, 128), ('gx', 'gy'), 0, 0, tiled=T...  9.18 us
    pallas_call x1, Pallas kernels, local(): pl.pallas_call(sums_body, out_shape=(f32(plane), f32(plane), f32((devices...  7.03 us
    ppermute x2, starting transfers between devices, ring_shift(): lax.ppermute(value, axis, [(i, (i + steps) % count) for i in range(count)])  6.69 us
    ppermute x2, waiting for transfers between devices, ring_shift(): lax.ppermute(value, axis, [(i, (i + steps) % count) for i in range(count)])  3.72 us
    pallas_call x1, Pallas kernels, local(): pl.pallas_call(remap_body, out_shape=(f32((tracers, *plane)), f32(plane))...  3.7 us
    pallas_call x1, Pallas kernels, local(): pl.pallas_call(pack_body, out_shape=(f32((4, layers, columns)), f32((laye...  2.76 us
    add x1, other arithmetic, local(): tracers_out = tracer_new + (totals[:tracers] / total)[:, None, None, None]  2.28 us
  transfers between devices with their start and end apart: 3, of which 2 were waited for; matrix products, arithmetic and copies ran while one was open for 0% of the time, Pallas kernels for 7%

profile of v1, /device:TPU:1, one launch (start us, length us, event | category | flops | bytes accessed | tf_op | source)
XLA Modules:
  0.0 54.9 jit_solution(142618142147854435)
XLA Ops:
  0.6 2.8 %pack_halo.1 = (f32[4,120,128]{2,1,0:T(8,128)}, f32[120,128]{1,0:T(8,128)}) custom-call(f32[2,120,128]{2,1,0:T(8,128)} %depth_ref.5, s32[2,120,128]{2,1,0:T(8,128)} %level_ref.5, bf16[2,120,128]{2,1,0:T(8,128)(2,1)} %start_ref.5, bf16[2,120,128]{2,1,0:T(8,128)(2,1)} %end_ref.5), custom_call_target="tpu_custom_call" | custom-call | flops 100000 | bytes 600000 | tf_op jit(solution)/shard_map/pack_halo/pallas_call | solution.py:367
  3.4 3.2 %collective-permute-start = (f32[4,120,128]{2,1,0:T(8,128)}, f32[4,120,128]{2,1,0:T(8,128)S(1)}, u32[]{:S(2)}, u32[]{:S(2)}) collective-permute-start(f32[4,120,128]{2,1,0:T(8,128)} %get-tuple-element.12), channel_id=1, source_target_pairs={{0,31},{1,0},{2,1},{3,2},{4,3},{5,4},{6,5},{7,6},{8,7},{9,8},{10,9... | collective-permute-start | bytes 737288 | tf_op jit(solution)/shard_map/ppermute | solution.py:343
  6.6 3.5 %collective-permute-start.1 = (f32[120,128]{1,0:T(8,128)}, f32[120,128]{1,0:T(8,128)S(1)}, u32[]{:S(2)}, u32[]{:S(2)}) collective-permute-start(f32[120,128]{1,0:T(8,128)} %get-tuple-element.13), channel_id=1, source_target_pairs={{0,224},{32,0},{64,32},{96,64},{128,96},{160,128},{192,160},{224,1... | collective-permute-start | bytes 184328 | tf_op jit(solution)/shard_map/ppermute | solution.py:343
  10.1 3.7 %collective-permute-done.1.column_ref = f32[120,128]{1,0:T(8,128)S(1)} collective-permute-done((f32[120,128]{1,0:T(8,128)}, f32[120,128]{1,0:T(8,128)S(1)}, u32[]{:S(2)}, u32[]{:S(2)}) %collective-permute-start.1) | collective-permute-done | bytes 61472 | tf_op jit(solution)/shard_map/ppermute | solution.py:343
  13.8 0.0 copy-start.2
  13.8 0.0 collective-permute-done.row_ref
  13.8 0.6 %copy-done.2 = f32[120,128]{1,0:T(8,128)} copy-done((f32[120,128]{1,0:T(8,128)}, f32[120,128]{1,0:T(8,128)S(1)}, u32[]{:S(2)}) %copy-start.2) | copy-done | bytes 61464
  14.4 0.0 copy-start
  14.4 0.7 %copy-done = f32[4,120,128]{2,1,0:T(8,128)} copy-done((f32[4,120,128]{2,1,0:T(8,128)}, f32[4,120,128]{2,1,0:T(8,128)S(1)}, u32[]{:S(2)}) %copy-start) | copy-done | bytes 245784
  15.1 7.0 %wind_and_sums.1 = (f32[2,120,128]{2,1,0:T(8,128)}, f32[2,120,128]{2,1,0:T(8,128)}, f32[256,128]{1,0:T(8,128)}) custom-call(bf16[8,2,120,128]{3,2,1,0:T(8,128)(2,1)} %species_ref.3, f32[2,120,128]{2,1,0:T(8,128)} %zonal_ref.1, f32[2,120,128]{2,1,0:T(8,128)} %merid_ref.1, f32[2,120,128]{2,1,0:T(8,128)} %warmth_ref.3, f32[2,120,128]{2,1,0:T(8,128)} %depth_ref.5, ...), custom_call_target="tpu_custom_call" | custom-call | flops 20000000 | bytes 2000000 | tf_op jit(solution)/shard_map/wind_and_sums/pallas_call | solution.py:377
  22.1 14.0 %all-to-all-start = ((f32[256,1,128]{2,1,0:T(1,128)}), f32[256,1,128]{2,1,0:T(1,128)S(1)}, u32[]{:S(2)}, u32[]{:S(2)}) async-start(f32[256,1,128]{2,1,0:T(1,128)} %bitcast.5), calls=%async_computation | async-start | bytes 262144 | tf_op jit(solution)/shard_map/all_to_all | solution.py:396
  36.1 3.7 %tracer_remap.1 = (f32[8,2,120,128]{3,2,1,0:T(8,128)}, f32[2,120,128]{2,1,0:T(8,128)}) custom-call(bf16[8,2,120,128]{3,2,1,0:T(8,128)(2,1)} %species_ref.3, f32[2,120,128]{2,1,0:T(8,128)} %warmth_ref.3, f32[2,120,128]{2,1,0:T(8,128)} %depth_ref.5, s32[2,120,128]{2,1,0:T(8,128)} %level_ref.5, bf16[2,120,128]{2,1,0:T(8,128)(2,1)} %start_ref.5, ...), custom_call_target="tpu_custom_call" | custom-call | flops 20000000 | bytes 2000000 | tf_op jit(solution)/shard_map/tracer_remap/pallas_call | solution.py:399
  39.8 0.0 copy-start.1
  39.8 9.2 %all-to-all-done = f32[256,1,128]{2,1,0:T(1,128)S(1)} async-done(((f32[256,1,128]{2,1,0:T(1,128)}), f32[256,1,128]{2,1,0:T(1,128)S(1)}, u32[]{:S(2)}, u32[]{:S(2)}) %all-to-all-start) | async-done | bytes 131104 | tf_op jit(solution)/shard_map/all_to_all | solution.py:396
  49.0 0.3 reduce_sum.9
  49.3 0.7 %fusion = (f32[1]{0:T(128)}, f32[1]{0:T(128)}) fusion(f32[128]{0:T(128)S(1)} %reduce_sum.9), kind=kLoop, calls=%fused_computation.3 | loop fusion | bytes 16 | tf_op jit(solution)/shard_map/slice | solution.py:414
  50.0 0.6 %slice_divide_fusion = f32[8]{0:T(128)S(1)} fusion(f32[128]{0:T(128)S(1)} %reduce_sum.9, f32[]{:T(128)} %bitcast.2), kind=kLoop, calls=%fused_computation.2 | loop fusion | flops 8 | bytes 68 | tf_op jit(solution)/shard_map/div | solution.py:413
  51.9 0.0 copy-done.1
  51.9 0.7 %broadcast_add_fusion.1 = f32[2,120,128]{2,1,0:T(8,128)} fusion(f32[2,120,128]{2,1,0:T(8,128)S(1)} %copy-done.1, f32[]{:T(128)S(6)} %div.11), kind=kLoop, calls=%fused_computation.1 | loop fusion | flops 30720 | bytes 245764 | tf_op jit(solution)/shard_map/add | solution.py:414
  52.6 2.3 %broadcast_add_fusion = f32[8,2,120,128]{3,2,1,0:T(8,128)} fusion(f32[8,2,120,128]{3,2,1,0:T(8,128)} %get-tuple-element.11, f32[8]{0:T(128)S(1)} %slice_divide_fusion), kind=kLoop, calls=%fused_computation | loop fusion | flops 245760 | bytes 1966112 | tf_op jit(solution)/shard_map/add | solution.py:413
Async XLA Ops:
  3.4 10.4 %collective-permute-start = (f32[4,120,128]{2,1,0:T(8,128)}, f32[4,120,128]{2,1,0:T(8,128)S(1)}, u32[]{:S(2)}, u32[]{:S(2)}) collective-permute-start(f32[4,120,128]{2,1,0:T(8,128)} %get-tuple-element.12), channel_id=1, source_target_pairs={{0,31},{1,0},{2,1},{3,2},{4,3},{5,4},{6,5},{7,6},{8,7},{9,8},{10,9... | collective-permute-start | bytes 737288 | tf_op jit(solution)/shard_map/ppermute | solution.py:343
  6.6 7.2 %collective-permute-start.1 = (f32[120,128]{1,0:T(8,128)}, f32[120,128]{1,0:T(8,128)S(1)}, u32[]{:S(2)}, u32[]{:S(2)}) collective-permute-start(f32[120,128]{1,0:T(8,128)} %get-tuple-element.13), channel_id=1, source_target_pairs={{0,224},{32,0},{64,32},{96,64},{128,96},{160,128},{192,160},{224,1... | collective-permute-start | bytes 184328 | tf_op jit(solution)/shard_map/ppermute | solution.py:343
  13.8 0.6 %copy-start.2 = (f32[120,128]{1,0:T(8,128)}, f32[120,128]{1,0:T(8,128)S(1)}, u32[]{:S(2)}) copy-start(f32[120,128]{1,0:T(8,128)S(1)} %collective-permute-done.1.column_ref) | copy-start | bytes 184324
  14.4 0.7 %copy-start = (f32[4,120,128]{2,1,0:T(8,128)}, f32[4,120,128]{2,1,0:T(8,128)S(1)}, u32[]{:S(2)}) copy-start(f32[4,120,128]{2,1,0:T(8,128)S(1)} %collective-permute-done.row_ref) | copy-start | bytes 737284
  22.1 26.9 %all-to-all-start = ((f32[256,1,128]{2,1,0:T(1,128)}), f32[256,1,128]{2,1,0:T(1,128)S(1)}, u32[]{:S(2)}, u32[]{:S(2)}) async-start(f32[256,1,128]{2,1,0:T(1,128)} %bitcast.5), calls=%async_computation | async-start | bytes 262144 | tf_op jit(solution)/shard_map/all_to_all | solution.py:396
  39.8 12.1 %copy-start.1 = (f32[2,120,128]{2,1,0:T(8,128)S(1)}, f32[2,120,128]{2,1,0:T(8,128)}, u32[]{:S(2)}) copy-start(f32[2,120,128]{2,1,0:T(8,128)} %get-tuple-element.17) | copy-start | bytes 368644

commit v2 on v1

v2 whole, which is shorter than its diff:
```python
import functools

import jax
import jax.numpy as jnp
from jax import lax
from jax.experimental import pallas as pl
from jax.experimental.pallas import tpu as pltpu
from jax.sharding import PartitionSpec as P

HEAT = 3.5
PAD = 8
STEP = 8
DIAGONALS = tuple(range(-4, 6))
C7 = 7.0 / 12.0
C1 = 1.0 / 12.0


def block_of(k):
    return pl.ds(pl.multiple_of(k * STEP, STEP), STEP)


def padded_block(k):
    return pl.ds(pl.multiple_of(k * STEP + PAD, STEP), STEP)


def shifted(ref, k, *lead):
    return lambda d: ref[(*lead, pl.ds(k * STEP + (PAD + d), STEP), slice(None))]


def layers_of(k):
    return lax.broadcasted_iota(jnp.int32, (STEP, 128), 0) + k * STEP


def clear_pads(ref, layers):
    lead = ref.shape[:-2]
    zero = jnp.zeros(lead + (PAD, ref.shape[-1]), ref.dtype)
    every = (slice(None),) * len(lead)
    ref[(*every, pl.ds(0, PAD), slice(None))] = zero
    ref[(*every, pl.ds(PAD + layers, PAD), slice(None))] = zero


def pick(masks, values):
    chosen = values[-1]
    for mask, value in zip(masks[-2::-1], values[-2::-1]):
        chosen = jnp.where(mask, value, chosen)
    return chosen


def operator(depth, level, start, end, target, layers):
    offset = level - target
    masks = [offset == o for o in (-2, -1, 0, 1, 2)]
    depths = [depth(d) for d in range(-2, 4)]
    weight_first = (1.0 - start) * pick(masks, depths[0:5])
    weight_second = end * pick(masks, depths[1:6])
    thick = weight_first + weight_second
    inverse = 1.0 / thick
    first = weight_first * inverse
    second = weight_second * inverse
    linear_first = 0.5 * (start + 1.0)
    square_first = linear_first - (start * start + start + 1.0) * (1.0 / 3.0)
    linear_second = 0.5 * end
    square_second = linear_second - end * end * (1.0 / 3.0)
    triple_first = 3.0 * square_first
    triple_second = 3.0 * square_second
    edge0 = first * (1.0 - linear_first - triple_first)
    edge1 = first * (linear_first - triple_first) + second * (
        1.0 - linear_second - triple_second
    )
    edge2 = second * (linear_second - triple_second)
    mean0 = first * (2.0 * triple_first)
    mean1 = second * (2.0 * triple_second)
    top, under_top = level == 0, level == 1
    bottom, over_bottom = level == layers - 2, level == layers - 3
    e0 = (
        jnp.where(top | under_top, 0.0, -C1),
        jnp.where(top, 0.0, jnp.where(under_top, 0.5, C7)),
        jnp.where(top, 1.5, jnp.where(under_top, 0.5, C7)),
        jnp.where(top, -0.5, jnp.where(under_top, 0.0, -C1)),
    )
    outer = jnp.where(top | bottom, 0.0, -C1)
    inner = jnp.where(top | bottom, 0.5, C7)
    e2 = (
        jnp.where(bottom, -0.5, jnp.where(over_bottom, 0.0, -C1)),
        jnp.where(bottom, 1.5, jnp.where(over_bottom, 0.5, C7)),
        jnp.where(bottom, 0.0, jnp.where(over_bottom, 0.5, C7)),
        jnp.where(bottom | over_bottom, 0.0, -C1),
    )
    taps = {
        -2: e0[0] * edge0,
        -1: e0[1] * edge0 + outer * edge1,
        0: e0[2] * edge0 + inner * edge1 + e2[0] * edge2 + mean0,
        1: e0[3] * edge0 + inner * edge1 + e2[1] * edge2 + mean1,
        2: outer * edge1 + e2[2] * edge2,
        3: e2[3] * edge2,
    }
    diagonals = []
    for d in DIAGONALS:
        value = jnp.zeros_like(thick)
        for mask, o in zip(masks, (-2, -1, 0, 1, 2)):
            if d - o in taps:
                value = jnp.where(mask, taps[d - o], value)
        diagonals.append(value)
    return thick, diagonals


def apply_operator(diagonals, values):
    total = None
    for d, weight in zip(DIAGONALS, diagonals):
        term = weight * values(d)
        total = term if total is None else total + term
    return total


def pack_body(
    depth_ref, level_ref, start_ref, end_ref, merid_ref, row_ref, send_ref, keep_ref, columns_s
):
    rows, layers, _ = depth_ref.shape
    lane = lax.broadcasted_iota(jnp.int32, (STEP, 128), 1)

    def step(k, carry):
        block = block_of(k)
        packed = jnp.zeros((STEP, 128), jnp.float32)
        for i, ref in enumerate((depth_ref, level_ref, start_ref, end_ref)):
            for r in range(rows):
                value = ref[r, block, :].astype(jnp.float32)
                if r == 0:
                    row_ref[i, block, :] = value
                place = i * rows + r
                if place:
                    value = pltpu.roll(value, place, 1)
                packed = jnp.where(lane == place, value, packed)
        for i, ref in enumerate((merid_ref, depth_ref)):
            for r in range(rows):
                place = STEP + i * rows + r
                packed = jnp.where(lane == place, pltpu.roll(ref[r, block, :], place + 1, 1), packed)
        columns_s[block, :] = packed
        return carry

    lax.fori_loop(0, layers // STEP, step, 0)
    columns_s[pl.ds(layers, 128 - layers), :] = jnp.zeros((128 - layers, 128), jnp.float32)
    across = columns_s[...].T
    send_ref[...] = across[0:STEP]
    keep_ref[...] = across[STEP : 2 * STEP]


def own_body(
    species_ref,
    zonal_ref,
    merid_ref,
    warmth_ref,
    depth_ref,
    level_ref,
    start_ref,
    end_ref,
    zonal_out,
    merid_out,
    last_out,
    edge_out,
    sums_out,
    depth_pad,
    zonal_pad,
    merid_pad,
    west_pad,
    adjoint_pad,
    thick_s,
    across_s,
    cross_s,
    columns_s,
):
    tracers = species_ref.shape[0]
    rows, layers, _ = depth_ref.shape
    blocks = layers // STEP
    for ref in (depth_pad, zonal_pad, merid_pad, west_pad, adjoint_pad):
        clear_pads(ref, layers)
    lane = lax.broadcasted_iota(jnp.int32, (STEP, 128), 1)

    def spread(k, carry):
        block, target = block_of(k), padded_block(k)
        for r in range(rows):
            depth_pad[r, target, :] = depth_ref[r, block, :]
            zonal_pad[r, target, :] = zonal_ref[r, block, :]
            value = merid_ref[r, block, :]
            merid_pad[r, target, :] = value
            west_pad[r, target, :] = pltpu.roll(value, 1, 1)
        return carry

    lax.fori_loop(0, blocks, spread, 0)

    def own(k, carry):
        block, target = block_of(k), padded_block(k)
        columns = jnp.zeros((STEP, 128), jnp.float32)
        for r in range(rows):
            thick, diagonals = operator(
                shifted(depth_pad, k, r),
                level_ref[r, block, :],
                start_ref[r, block, :].astype(jnp.float32),
                end_ref[r, block, :].astype(jnp.float32),
                layers_of(k),
                layers,
            )
            thick_s[r, block, :] = thick
            zonal_out[r, block, :] = apply_operator(diagonals, shifted(zonal_pad, k, r))
            merid = apply_operator(diagonals, shifted(merid_pad, k, r))
            merid_out[r, block, :] = merid
            across_s[r, block, :] = apply_operator(diagonals, shifted(west_pad, k, r))
            if r:
                cross_s[r - 1, block, :] = apply_operator(
                    diagonals, shifted(zonal_pad, k, r - 1)
                )
            for i, weight in enumerate(diagonals):
                adjoint_pad[r, i, target, :] = thick * weight
            for i, value in enumerate((thick, merid)):
                place = i * rows + r
                columns = jnp.where(lane == place, pltpu.roll(value, place + 1, 1), columns)
        columns_s[block, :] = columns
        return carry

    lax.fori_loop(0, blocks, own, 0)
    columns_s[pl.ds(layers, 128 - layers), :] = jnp.zeros((128 - layers, 128), jnp.float32)
    edge_out[...] = columns_s[...].T[0:STEP]

    def totals(k, carry):
        block = block_of(k)
        masses, energy, total = list(carry[:-2]), carry[-2], carry[-1]
        for r in range(rows):
            depth = depth_ref[r, block, :]
            back = None
            for i, d in enumerate(DIAGONALS):
                term = adjoint_pad[r, i, pl.ds(k * STEP + (PAD - d), STEP), :]
                back = term if back is None else back + term
            lost = depth - back
            for t in range(tracers):
                masses[t] = masses[t] + species_ref[t, r, block, :].astype(jnp.float32) * lost
            energy = energy + HEAT * (warmth_ref[r, block, :] * lost)
            thick = thick_s[r, block, :]
            total = total + thick
            if r + 1 < rows:
                zonal = 0.5 * (zonal_out[r, block, :] + cross_s[r, block, :])
                zonal_out[r, block, :] = zonal
                wind = zonal_ref[r, block, :]
                energy = energy + 0.25 * (
                    (depth + depth_ref[r + 1, block, :]) * (wind * wind)
                    - (thick + thick_s[r + 1, block, :]) * (zonal * zonal)
                )
            else:
                last_out[0, block, :] = zonal_ref[r, block, :]
                last_out[1, block, :] = depth
                last_out[2, block, :] = thick
            merid = 0.5 * (merid_out[r, block, :] + pltpu.roll(across_s[r, block, :], 127, 1))
            merid_out[r, block, :] = merid
            wind = merid_ref[r, block, :]
            kinetic = (depth + pltpu.roll(depth, 127, 1)) * (wind * wind) - (
                thick + pltpu.roll(thick, 127, 1)
            ) * (merid * merid)
            energy = energy + jnp.where(lane == 127, 0.0, 0.25 * kinetic)
        return (*masses, energy, total)

    zero = jnp.zeros((STEP, 128), jnp.float32)
    parts = lax.fori_loop(0, blocks, totals, (zero,) * (tracers + 2))
    for i, part in enumerate(parts):
        sums_out[i] = part


def halo_body(
    row_ref,
    column_ref,
    keep_ref,
    zonal_ref,
    last_ref,
    edge_ref,
    parts_ref,
    zonal_out,
    merid_out,
    sums_out,
    depth_pad,
    zonal_pad,
):
    layers = row_ref.shape[1]
    rows = zonal_ref.shape[0]
    blocks = layers // STEP
    clear_pads(depth_pad, layers)
    clear_pads(zonal_pad, layers)
    lane = lax.broadcasted_iota(jnp.int32, (STEP, 128), 1)
    sublane = lax.broadcasted_iota(jnp.int32, (STEP, 128), 0)

    packed = column_ref[...]
    thick, diagonals = operator(
        lambda d: pltpu.roll(packed, -d % 128, 1),
        pltpu.roll(packed, STEP - rows, 0).astype(jnp.int32),
        pltpu.roll(packed, STEP - 2 * rows, 0),
        pltpu.roll(packed, STEP - 3 * rows, 0),
        lane,
        layers,
    )
    wind = keep_ref[...]
    depth = pltpu.roll(wind, STEP - rows, 0)
    edge = edge_ref[...]
    merid = 0.5 * (
        pltpu.roll(edge, STEP - rows, 0)
        + apply_operator(diagonals, lambda d: pltpu.roll(wind, -d % 128, 1))
    )
    merid_out[...] = merid
    kinetic = (depth + packed) * (wind * wind) - (edge + thick) * (merid * merid)
    energy = jnp.where((lane < layers) & (sublane < rows), 0.25 * kinetic, 0.0)

    def spread(k, carry):
        block, target = block_of(k), padded_block(k)
        depth_pad[target, :] = row_ref[0, block, :]
        zonal_pad[target, :] = last_ref[0, block, :]
        return carry

    lax.fori_loop(0, blocks, spread, 0, unroll=5)

    def north(k, energy):
        block = block_of(k)
        thick, diagonals = operator(
            shifted(depth_pad, k),
            row_ref[1, block, :].astype(jnp.int32),
            row_ref[2, block, :],
            row_ref[3, block, :],
            layers_of(k),
            layers,
        )
        zonal = 0.5 * (
            zonal_ref[rows - 1, block, :] + apply_operator(diagonals, shifted(zonal_pad, k))
        )
        zonal_out[block, :] = zonal
        wind = last_ref[0, block, :]
        return energy + 0.25 * (
            (last_ref[1, block, :] + row_ref[0, block, :]) * (wind * wind)
            - (last_ref[2, block, :] + thick) * (zonal * zonal)
        )

    energy = lax.fori_loop(0, blocks, north, energy)
    row = jnp.zeros((STEP, 128), jnp.float32)
    count = parts_ref.shape[0]
    for i in range(count):
        part = parts_ref[i]
        if i == count - 2:
            part = part + energy
        row = jnp.where(lane == i, jnp.sum(part, axis=1, keepdims=True), row)
    row = jnp.sum(row, axis=0, keepdims=True)
    sums_out[...] = jnp.broadcast_to(row, sums_out.shape)


def remap_body(
    species_ref,
    warmth_ref,
    depth_ref,
    level_ref,
    start_ref,
    end_ref,
    zonal_ref,
    last_ref,
    merid_ref,
    edge_ref,
    tracers_out,
    warmth_out,
    zonal_out,
    merid_out,
    depth_pad,
    field_pad,
    columns_s,
):
    tracers = species_ref.shape[0]
    rows, layers, _ = depth_ref.shape
    blocks = layers // STEP
    clear_pads(depth_pad, layers)
    clear_pads(field_pad, layers)
    lane = lax.broadcasted_iota(jnp.int32, (STEP, 128), 1)
    columns_s[...] = jnp.zeros_like(columns_s)
    columns_s[0:STEP, :] = edge_ref[...]
    columns_s[...] = columns_s[...].T

    def spread(k, carry):
        block, target = block_of(k), padded_block(k)
        edge = columns_s[block, :]
        for r in range(rows):
            depth_pad[r, target, :] = depth_ref[r, block, :]
            field_pad[tracers, r, target, :] = warmth_ref[r, block, :]
            for t in range(tracers):
                field_pad[t, r, target, :] = species_ref[t, r, block, :].astype(jnp.float32)
            zonal_out[r, block, :] = (
                zonal_ref[r, block, :] if r + 1 < rows else last_ref[block, :]
            )
            merid_out[r, block, :] = jnp.where(
                lane == 127, pltpu.roll(edge, 127 - r, 1), merid_ref[r, block, :]
            )
        return carry

    lax.fori_loop(0, blocks, spread, 0)

    def own(k, carry):
        block = block_of(k)
        for r in range(rows):
            _, diagonals = operator(
                shifted(depth_pad, k, r),
                level_ref[r, block, :],
                start_ref[r, block, :].astype(jnp.float32),
                end_ref[r, block, :].astype(jnp.float32),
                layers_of(k),
                layers,
            )
            for t in range(tracers):
                tracers_out[t, r, block, :] = apply_operator(
                    diagonals, shifted(field_pad, k, t, r)
                )
            warmth_out[r, block, :] = apply_operator(
                diagonals, shifted(field_pad, k, tracers, r)
            )
        return carry

    lax.fori_loop(0, blocks, own, 0)


def correct_body(gathered_ref, tracer_ref, warmth_ref, tracers_out, warmth_out, new_s, heat_s, sem):
    tracers = tracer_ref.shape[0]
    totals = jnp.sum(gathered_ref[...], axis=0, keepdims=True)
    total = totals[:, tracers + 1 : tracers + 2]
    scale = 1.0 / total
    copies = []
    for t in range(tracers):
        new_s[t] = tracer_ref[t] + totals[:, t : t + 1] * scale
        copies.append(pltpu.make_async_copy(new_s.at[t], tracers_out.at[t], sem.at[t]))
        copies[-1].start()
    heat_s[...] = warmth_ref[...] + totals[:, tracers : tracers + 1] * (scale * (1.0 / HEAT))
    copies.append(pltpu.make_async_copy(heat_s, warmth_out, sem.at[tracers]))
    copies[-1].start()
    for copy in copies:
        copy.wait()


def ring_shift(value, axis, steps):
    count = lax.axis_size(axis)
    return lax.ppermute(value, axis, [(i, (i + steps) % count) for i in range(count)])


def kernel(body, name, flops, moved, scratch, near, outs, operands):
    operands = [
        pltpu.with_memory_space_constraint(x, pltpu.VMEM if i in near else pltpu.HBM)
        for i, x in enumerate(operands)
    ]
    vmem = pl.BlockSpec(memory_space=pltpu.VMEM)
    hbm = pl.BlockSpec(memory_space=pl.ANY)
    return pl.pallas_call(
        body,
        out_shape=tuple(
            pltpu.VMEM(shape, jnp.float32)
            if place == "vmem"
            else jax.ShapeDtypeStruct(shape, jnp.float32)
            for shape, place in outs
        ),
        in_specs=[vmem] * len(operands),
        out_specs=tuple(hbm if place == "any" else vmem for _, place in outs),
        scratch_shapes=scratch,
        cost_estimate=pl.CostEstimate(flops=flops, bytes_accessed=moved, transcendentals=0),
        compiler_params=pltpu.CompilerParams(vmem_limit_bytes=24 * 2**20),
        name=name,
    )(*operands)


def local(species, zonal, merid, warmth, depth, level, start, end):
    tracers = species.shape[0]
    plane = rows, layers, columns = depth.shape
    devices = lax.axis_size(("gx", "gy"))
    tall = layers + 2 * PAD
    tile = (STEP, 128)
    real = functools.partial(pltpu.VMEM, dtype=jnp.float32)
    row_halo, column_halo, keep = kernel(
        pack_body,
        "pack_halo",
        100_000,
        600_000,
        [real((128, 128))],
        (),
        [((4, layers, columns), "vmem"), (tile, "vmem"), (tile, "vmem")],
        (depth, level, start, end, merid),
    )
    row_halo = ring_shift(row_halo, "gy", -1)
    column_halo = ring_shift(column_halo, "gx", -1)
    zonal_part, merid_part, last, edge, parts = kernel(
        own_body,
        "own_columns",
        20_000_000,
        2_000_000,
        [
            real((rows, tall, columns)),
            real((rows, tall, columns)),
            real((rows, tall, columns)),
            real((rows, tall, columns)),
            real((rows, len(DIAGONALS), tall, columns)),
            real(plane),
            real(plane),
            real(plane),
            real((128, 128)),
        ],
        (),
        [
            (plane, "vmem"),
            (plane, "vmem"),
            ((3, layers, columns), "vmem"),
            (tile, "vmem"),
            ((tracers + 2, *tile), "vmem"),
        ],
        (species, zonal, merid, warmth, depth, level, start, end),
    )
    zonal_last, merid_last, sums = kernel(
        halo_body,
        "halo_faces",
        2_000_000,
        500_000,
        [real((tall, columns)), real((tall, columns))],
        range(7),
        [((layers, columns), "vmem"), (tile, "vmem"), ((devices, 128), "vmem")],
        (row_halo, column_halo, keep, zonal_part, last, edge, parts),
    )
    gathered = lax.all_to_all(sums.reshape(devices, 1, 128), ("gx", "gy"), 0, 0, tiled=True)
    tracer_new, warmth_new, zonal_new, merid_new = kernel(
        remap_body,
        "tracer_remap",
        20_000_000,
        2_000_000,
        [
            real((rows, tall, columns)),
            real((tracers + 1, rows, tall, columns)),
            real((128, 128)),
        ],
        range(6, 10),
        [((tracers, *plane), "vmem"), (plane, "vmem"), (plane, "hbm"), (plane, "hbm")],
        (species, warmth, depth, level, start, end, zonal_part, zonal_last, merid_part, merid_last),
    )
    tracers_out, warmth_out = kernel(
        correct_body,
        "corrections",
        1_000_000,
        2_000_000,
        [real((tracers, *plane)), real(plane), pltpu.SemaphoreType.DMA((tracers + 1,))],
        range(3),
        [((tracers, *plane), "any"), (plane, "any")],
        (gathered.reshape(devices, 128), tracer_new, warmth_new),
    )
    return tracers_out, zonal_new, merid_new, warmth_out


def solution(mesh):
    plane = P("gy", None, "gx")
    stack = P(None, "gy", None, "gx")
    return jax.shard_map(
        local,
        mesh=mesh,
        in_specs=(stack,) + (plane,) * 7,
        out_specs=(stack, plane, plane, plane),
        check_vma=False,
    )
```

time: 55.1 us -> 42.2 us (0.77)
  waiting for transfers between devices: 12.9 us -> 8.56 us
  other arithmetic: 3.85 us -> 0 us
  starting transfers between devices: 20.7 us -> 18 us
  local copies, waits for them, and re-layouts: 1.97 us -> 0 us
  Pallas kernels: 13.5 us -> 14.9 us
  between operations: 1.98 us -> 0.66 us
    ppermute x2, waiting for transfers between devices: 3.72 us -> 0.01 us  [ring_shift(): lax.ppermute(value, axis, [(i, (i + steps) % count) for i in range(count)])]
    add x2 -> x0, other arithmetic: 2.94 us -> none  [the longest x1 2.28 us: local(): tracers_out = tracer_new + (totals[:tracers] / total)[:, None, None, None]]
    all_to_all x1, starting transfers between devices: 14 us -> 11.2 us  [local(): lax.all_to_all(sums.reshape(devices, 1, 128), ('gx', 'gy'), 0, 0, tiled=T...]
    pallas_call x3 -> x5, Pallas kernels: 13.5 us -> 14.9 us  [kernel(): pl.pallas_call(body, out_shape=tuple((pltpu.VMEM(shape, jnp.float32) if p...]
    unnamed x6 -> x0, local copies, waits for them, and re-layouts: 1.32 us -> none
    slice x1 -> x0, local copies, waits for them, and re-layouts: 0.65 us -> none  [local(): warmth_out = warmth_new + totals[tracers] / (HEAT * total)]
    div x1 -> x0, other arithmetic: 0.63 us -> none  [local(): tracers_out = tracer_new + (totals[:tracers] / total)[:, None, None, None]]
    all_to_all x1, waiting for transfers between devices: 9.18 us -> 8.56 us  [local(): lax.all_to_all(sums.reshape(devices, 1, 128), ('gx', 'gy'), 0, 0, tiled=T...]
  transfers between devices with their start and end apart: 3 -> 3, of which waited for: 2 -> 1; matrix products, arithmetic and copies ran while one was open for 0% -> 0% of each run, Pallas kernels for 7% -> 23%
where the time goes in v2:
time: 42.2 us; the launch traced here: 42.1 us
  starting transfers between devices  18 us (43%)
  Pallas kernels  14.9 us (35%)
  waiting for transfers between devices  8.56 us (20%)
  between operations  0.66 us (2%)
    pallas_call x5, Pallas kernels, kernel(): pl.pallas_call(body, out_shape=tuple((pltpu.VMEM(shape, jnp.float32) if p...  14.9 us
    all_to_all x1, starting transfers between devices, local(): lax.all_to_all(sums.reshape(devices, 1, 128), ('gx', 'gy'), 0, 0, tiled=T...  11.2 us
    all_to_all x1, waiting for transfers between devices, local(): lax.all_to_all(sums.reshape(devices, 1, 128), ('gx', 'gy'), 0, 0, tiled=T...  8.56 us
    ppermute x2, starting transfers between devices, ring_shift(): lax.ppermute(value, axis, [(i, (i + steps) % count) for i in range(count)])  6.74 us
  transfers between devices with their start and end apart: 3, of which 1 were waited for; matrix products, arithmetic and copies ran while one was open for 0% of the time, Pallas kernels for 23%

profile of v2, /device:TPU:1, one launch (start us, length us, event | category | flops | bytes accessed | tf_op | source)
XLA Modules:
  0.0 42.1 jit_solution(4498711630894729572)
XLA Ops:
  0.6 2.3 %pack_halo.1 = (f32[4,120,128]{2,1,0:T(8,128)S(1)}, f32[8,128]{1,0:T(8,128)S(1)}, f32[8,128]{1,0:T(8,128)S(1)}) custom-call(f32[2,120,128]{2,1,0:T(8,128)} %depth_ref.5, s32[2,120,128]{2,1,0:T(8,128)} %level_ref.5, bf16[2,120,128]{2,1,0:T(8,128)(2,1)} %start_ref.5, bf16[2,120,128]{2,1,0:T(8,128)(2,1)} %end_ref.5, f32[2,120,128]{2,1,0:T(8,128)} %merid_ref.3), custom_call_target="tpu_custom_call" | custom-call | flops 100000 | bytes 600000 | tf_op jit(solution)/shard_map/pack_halo/pallas_call | solution.py:445
  3.0 3.3 %collective-permute-start = (f32[4,120,128]{2,1,0:T(8,128)S(1)}, f32[4,120,128]{2,1,0:T(8,128)S(1)}, u32[]{:S(2)}, u32[]{:S(2)}) collective-permute-start(f32[4,120,128]{2,1,0:T(8,128)S(1)} %get-tuple-element.21), channel_id=1, source_target_pairs={{0,31},{1,0},{2,1},{3,2},{4,3},{5,4},{6,5},{7,6},{8,7},{9,8},{10,9... | collective-permute-start | bytes 737288 | tf_op jit(solution)/shard_map/ppermute | solution.py:435
  6.2 3.5 %collective-permute-start.1 = (f32[8,128]{1,0:T(8,128)S(1)}, f32[8,128]{1,0:T(8,128)S(1)}, u32[]{:S(2)}, u32[]{:S(2)}) collective-permute-start(f32[8,128]{1,0:T(8,128)S(1)} %get-tuple-element.22), channel_id=1, source_target_pairs={{0,224},{32,0},{64,32},{96,64},{128,96},{160,128},{192,160},{224,1... | collective-permute-start | bytes 12296 | tf_op jit(solution)/shard_map/ppermute | solution.py:435
  9.7 5.4 %own_columns.1 = (f32[2,120,128]{2,1,0:T(8,128)S(1)}, f32[2,120,128]{2,1,0:T(8,128)S(1)}, f32[3,120,128]{2,1,0:T(8,128)S(1)}, f32[8,128]{1,0:T(8,128)S(1)}, f32[10,8,128]{2,1,0:T(8,128)S(1)}) custom-call(bf16[8,2,120,128]{3,2,1,0:T(8,128)(2,1)} %species_ref.3, f32[2,120,128]{2,1,0:T(8,128)} %zonal_ref.1, f32[2,120,128]{2,1,0:T(8,128)} %merid_ref.3, ...), custom_call_target="tpu_custom_call" | custom-call | flops 20000000 | bytes 2000000 | tf_op jit(solution)/shard_map/own_columns/pallas_call | solution.py:445
  15.1 0.0 collective-permute-done.1.column_ref
  15.1 0.0 collective-permute-done.row_ref
  15.1 1.5 %halo_faces.1 = (f32[120,128]{1,0:T(8,128)S(1)}, f32[8,128]{1,0:T(8,128)S(1)}, f32[256,128]{1,0:T(8,128)}) custom-call(f32[4,120,128]{2,1,0:T(8,128)S(1)} %collective-permute-done.row_ref, f32[8,128]{1,0:T(8,128)S(1)} %collective-permute-done.1.column_ref, f32[8,128]{1,0:T(8,128)S(1)} %get-tuple-element.23.keep_ref, ...), custom_call_target="tpu_custom_call" | custom-call | flops 2000000 | bytes 500000 | tf_op jit(solution)/shard_map/halo_faces/pallas_call | solution.py:445
  16.6 11.2 %all-to-all-start = ((f32[256,1,128]{2,1,0:T(1,128)}), f32[256,1,128]{2,1,0:T(1,128)S(1)}, u32[]{:S(2)}, u32[]{:S(2)}) async-start(f32[256,1,128]{2,1,0:T(1,128)} %bitcast.1), calls=%async_computation | async-start | bytes 262144 | tf_op jit(solution)/shard_map/all_to_all | solution.py:517
  27.9 4.4 %tracer_remap.1 = (f32[8,2,120,128]{3,2,1,0:T(8,128)S(1)}, f32[2,120,128]{2,1,0:T(8,128)S(1)}, f32[2,120,128]{2,1,0:T(8,128)}, f32[2,120,128]{2,1,0:T(8,128)}) custom-call(bf16[8,2,120,128]{3,2,1,0:T(8,128)(2,1)} %species_ref.3, f32[2,120,128]{2,1,0:T(8,128)} %warmth_ref.3, f32[2,120,128]{2,1,0:T(8,128)} %depth_ref.5, s32[2,120,128]{2,1,0:T(8,128)} %level_ref.5, ...), custom_call_target="tpu_custom_call" | custom-call | flops 20000000 | bytes 2000000 | tf_op jit(solution)/shard_map/tracer_remap/pallas_call | solution.py:445
  32.3 8.6 %all-to-all-done = f32[256,1,128]{2,1,0:T(1,128)S(1)} async-done(((f32[256,1,128]{2,1,0:T(1,128)}), f32[256,1,128]{2,1,0:T(1,128)S(1)}, u32[]{:S(2)}, u32[]{:S(2)}) %all-to-all-start) | async-done | bytes 131104 | tf_op jit(solution)/shard_map/all_to_all | solution.py:517
  40.8 1.2 %corrections.1 = (f32[8,2,120,128]{3,2,1,0:T(8,128)}, f32[2,120,128]{2,1,0:T(8,128)}) custom-call(f32[256,128]{1,0:T(8,128)S(1)} %bitcast.4, f32[8,2,120,128]{3,2,1,0:T(8,128)S(1)} %get-tuple-element.32.tracer_ref, f32[2,120,128]{2,1,0:T(8,128)S(1)} %get-tuple-element.33.warmth_ref), custom_call_target="tpu_custom_call" | custom-call | flops 1000000 | bytes 2000000 | tf_op jit(solution)/shard_map/corrections/pallas_call | solution.py:445
Async XLA Ops:
  3.0 12.2 %collective-permute-start = (f32[4,120,128]{2,1,0:T(8,128)S(1)}, f32[4,120,128]{2,1,0:T(8,128)S(1)}, u32[]{:S(2)}, u32[]{:S(2)}) collective-permute-start(f32[4,120,128]{2,1,0:T(8,128)S(1)} %get-tuple-element.21), channel_id=1, source_target_pairs={{0,31},{1,0},{2,1},{3,2},{4,3},{5,4},{6,5},{7,6},{8,7},{9,8},{10,9... | collective-permute-start | bytes 737288 | tf_op jit(solution)/shard_map/ppermute | solution.py:435
  6.2 8.9 %collective-permute-start.1 = (f32[8,128]{1,0:T(8,128)S(1)}, f32[8,128]{1,0:T(8,128)S(1)}, u32[]{:S(2)}, u32[]{:S(2)}) collective-permute-start(f32[8,128]{1,0:T(8,128)S(1)} %get-tuple-element.22), channel_id=1, source_target_pairs={{0,224},{32,0},{64,32},{96,64},{128,96},{160,128},{192,160},{224,1... | collective-permute-start | bytes 12296 | tf_op jit(solution)/shard_map/ppermute | solution.py:435
  16.6 24.2 %all-to-all-start = ((f32[256,1,128]{2,1,0:T(1,128)}), f32[256,1,128]{2,1,0:T(1,128)S(1)}, u32[]{:S(2)}, u32[]{:S(2)}) async-start(f32[256,1,128]{2,1,0:T(1,128)} %bitcast.1), calls=%async_computation | async-start | bytes 262144 | tf_op jit(solution)/shard_map/all_to_all | solution.py:517

commit v3 on v2

v3 whole, which is shorter than its diff:
```python
import functools

import jax
import jax.numpy as jnp
from jax import lax
from jax.experimental import pallas as pl
from jax.experimental.pallas import tpu as pltpu
from jax.sharding import PartitionSpec as P


HEAT = 3.5
PAD = 8
STEP = 8
DIAGONALS = tuple(range(-4, 6))
C7 = 7.0 / 12.0
C1 = 1.0 / 12.0


def block_of(k, first=0):
    start = k * STEP + first
    return pl.ds(start if isinstance(k, int) else pl.multiple_of(start, STEP), STEP)


def padded_block(k):
    return block_of(k, PAD)


def shifted(ref, k, *lead):
    return lambda d: ref[(*lead, pl.ds(k * STEP + (PAD + d), STEP), slice(None))]


def layers_of(k):
    return lax.broadcasted_iota(jnp.int32, (STEP, 128), 0) + k * STEP


def clear_pads(ref, layers):
    lead = ref.shape[:-2]
    zero = jnp.zeros(lead + (PAD, ref.shape[-1]), ref.dtype)
    every = (slice(None),) * len(lead)
    ref[(*every, pl.ds(0, PAD), slice(None))] = zero
    ref[(*every, pl.ds(PAD + layers, PAD), slice(None))] = zero


def pick(masks, values):
    chosen = values[-1]
    for mask, value in zip(masks[-2::-1], values[-2::-1]):
        chosen = jnp.where(mask, value, chosen)
    return chosen


def operator(depth, level, start, end, target, layers):
    offset = level - target
    masks = [offset == o for o in (-2, -1, 0, 1, 2)]
    depths = [depth(d) for d in range(-2, 4)]
    weight_first = (1.0 - start) * pick(masks, depths[0:5])
    weight_second = end * pick(masks, depths[1:6])
    thick = weight_first + weight_second
    inverse = 1.0 / thick
    first = weight_first * inverse
    second = weight_second * inverse
    linear_first = 0.5 * (start + 1.0)
    square_first = linear_first - (start * start + start + 1.0) * (1.0 / 3.0)
    linear_second = 0.5 * end
    square_second = linear_second - end * end * (1.0 / 3.0)
    triple_first = 3.0 * square_first
    triple_second = 3.0 * square_second
    edge0 = first * (1.0 - linear_first - triple_first)
    edge1 = first * (linear_first - triple_first) + second * (
        1.0 - linear_second - triple_second
    )
    edge2 = second * (linear_second - triple_second)
    mean0 = first * (2.0 * triple_first)
    mean1 = second * (2.0 * triple_second)
    top, under_top = level == 0, level == 1
    bottom, over_bottom = level == layers - 2, level == layers - 3
    e0 = (
        jnp.where(top | under_top, 0.0, -C1),
        jnp.where(top, 0.0, jnp.where(under_top, 0.5, C7)),
        jnp.where(top, 1.5, jnp.where(under_top, 0.5, C7)),
        jnp.where(top, -0.5, jnp.where(under_top, 0.0, -C1)),
    )
    outer = jnp.where(top | bottom, 0.0, -C1)
    inner = jnp.where(top | bottom, 0.5, C7)
    e2 = (
        jnp.where(bottom, -0.5, jnp.where(over_bottom, 0.0, -C1)),
        jnp.where(bottom, 1.5, jnp.where(over_bottom, 0.5, C7)),
        jnp.where(bottom, 0.0, jnp.where(over_bottom, 0.5, C7)),
        jnp.where(bottom | over_bottom, 0.0, -C1),
    )
    taps = {
        -2: e0[0] * edge0,
        -1: e0[1] * edge0 + outer * edge1,
        0: e0[2] * edge0 + inner * edge1 + e2[0] * edge2 + mean0,
        1: e0[3] * edge0 + inner * edge1 + e2[1] * edge2 + mean1,
        2: outer * edge1 + e2[2] * edge2,
        3: e2[3] * edge2,
    }
    diagonals = []
    for d in DIAGONALS:
        value = jnp.zeros_like(thick)
        for mask, o in zip(masks, (-2, -1, 0, 1, 2)):
            if d - o in taps:
                value = jnp.where(mask, taps[d - o], value)
        diagonals.append(value)
    return thick, diagonals


def apply_operator(diagonals, values):
    total = None
    for d, weight in zip(DIAGONALS, diagonals):
        term = weight * values(d)
        total = term if total is None else total + term
    return total


def pack_body(depth_ref, level_ref, start_ref, end_ref, row_ref, send_ref, columns_s):
    rows, layers, columns = depth_ref.shape
    lane = lax.broadcasted_iota(jnp.int32, (layers, columns), 1)
    packed = jnp.zeros((layers, columns), jnp.float32)
    for i, ref in enumerate((depth_ref, level_ref, start_ref, end_ref)):
        for r in range(rows):
            value = ref[r].astype(jnp.float32)
            if r == 0:
                row_ref[i] = value
            place = i * rows + r
            if place:
                value = pltpu.roll(value, place, 1)
            packed = jnp.where(lane == place, value, packed)
    columns_s[pl.ds(0, layers), :] = packed
    columns_s[pl.ds(layers, 128 - layers), :] = jnp.zeros((128 - layers, 128), jnp.float32)
    send_ref[...] = columns_s[...].T[0:STEP]


def own_body(
    species_ref,
    zonal_ref,
    merid_ref,
    warmth_ref,
    depth_ref,
    level_ref,
    start_ref,
    end_ref,
    tracers_out,
    warmth_out,
    zonal_out,
    merid_out,
    last_out,
    edge_out,
    sums_out,
    depth_pad,
    zonal_pad,
    merid_pad,
    west_pad,
    field_pad,
    thick_s,
    across_s,
    columns_s,
):
    tracers = species_ref.shape[0]
    rows, layers, _ = depth_ref.shape
    blocks = layers // STEP
    for ref in (depth_pad, zonal_pad, merid_pad, west_pad, field_pad):
        clear_pads(ref, layers)

    def spread(k, carry):
        block, target = block_of(k), padded_block(k)
        for r in range(rows):
            depth_pad[r, target, :] = depth_ref[r, block, :]
            zonal_pad[r, target, :] = zonal_ref[r, block, :]
            merid_pad[r, target, :] = merid_ref[r, block, :]
            field_pad[tracers, r, target, :] = warmth_ref[r, block, :]
            for t in range(tracers):
                field_pad[t, r, target, :] = species_ref[t, r, block, :].astype(jnp.float32)
        return carry

    lax.fori_loop(0, blocks, spread, 0)
    for r in range(rows):
        west_pad[r, pl.ds(PAD, layers), :] = pltpu.roll(merid_ref[r], 1, 1)

    def own(k, carry):
        block, target = block_of(k), padded_block(k)
        lost, energy, total = list(carry[:-2]), carry[-2], carry[-1]
        thick_before = zonal_before = None
        for r in range(rows):
            thick, diagonals = operator(
                shifted(depth_pad, k, r),
                level_ref[r, block, :],
                start_ref[r, block, :].astype(jnp.float32),
                end_ref[r, block, :].astype(jnp.float32),
                layers_of(k),
                layers,
            )
            depth = depth_ref[r, block, :]
            thick_s[r, block, :] = thick
            total = total + thick
            merid_out[r, block, :] = apply_operator(diagonals, shifted(merid_pad, k, r))
            across_s[r, block, :] = apply_operator(diagonals, shifted(west_pad, k, r))
            for t in range(tracers):
                new = apply_operator(diagonals, shifted(field_pad, k, t, r))
                tracers_out[t, r, block, :] = new
                lost[t] = lost[t] + (depth * field_pad[t, r, target, :] - thick * new)
            new = apply_operator(diagonals, shifted(field_pad, k, tracers, r))
            warmth_out[r, block, :] = new
            energy = energy + HEAT * (depth * field_pad[tracers, r, target, :] - thick * new)
            zonal = apply_operator(diagonals, shifted(zonal_pad, k, r))
            if r:
                crossed = 0.5 * (
                    zonal_before + apply_operator(diagonals, shifted(zonal_pad, k, r - 1))
                )
                zonal_out[r - 1, block, :] = crossed
                wind = zonal_ref[r - 1, block, :]
                energy = energy + 0.25 * (
                    (depth_ref[r - 1, block, :] + depth) * (wind * wind)
                    - (thick_before + thick) * (crossed * crossed)
                )
            if r + 1 == rows:
                zonal_out[r, block, :] = zonal
                last_out[0, block, :] = zonal_ref[r, block, :]
                last_out[1, block, :] = depth
                last_out[2, block, :] = thick
            thick_before, zonal_before = thick, zonal
        return (*lost, energy, total)

    zero = jnp.zeros((STEP, 128), jnp.float32)
    parts = lax.fori_loop(0, blocks, own, (zero,) * (tracers + 2))

    lane = lax.broadcasted_iota(jnp.int32, (layers, 128), 1)
    columns = jnp.zeros((layers, 128), jnp.float32)
    shared = jnp.zeros((STEP, 128), jnp.float32)
    for r in range(rows):
        for i, ref in enumerate((thick_s, merid_out, depth_ref, merid_ref)):
            place = i * rows + r
            columns = jnp.where(lane == place, pltpu.roll(ref[r], place + 1, 1), columns)
        depth, thick, wind = depth_ref[r], thick_s[r], merid_ref[r]
        merid = 0.5 * (merid_out[r] + pltpu.roll(across_s[r], 127, 1))
        merid_out[r] = merid
        kinetic = (depth + pltpu.roll(depth, 127, 1)) * (wind * wind) - (
            thick + pltpu.roll(thick, 127, 1)
        ) * (merid * merid)
        shared = shared + jnp.sum(kinetic.reshape(blocks, STEP, 128), axis=0)
    columns_s[pl.ds(0, layers), :] = columns
    columns_s[pl.ds(layers, 128 - layers), :] = jnp.zeros((128 - layers, 128), jnp.float32)
    edge_out[...] = columns_s[...].T[0:STEP]

    lane = lax.broadcasted_iota(jnp.int32, (STEP, 128), 1)
    row = jnp.zeros((STEP, 128), jnp.float32)
    for i, part in enumerate(parts):
        if i != tracers:
            row = jnp.where(lane == i, jnp.sum(part, axis=1, keepdims=True), row)
    sums_out[0] = row
    sums_out[1] = parts[tracers] + jnp.where(lane == 127, 0.0, 0.25 * shared)


def north_faces(row_ref, zonal_ref, last_ref, energy, zonal_out, depth_pad, zonal_pad):
    layers = row_ref.shape[1]
    rows = zonal_ref.shape[0]
    clear_pads(depth_pad, layers)
    clear_pads(zonal_pad, layers)
    depth_pad[pl.ds(PAD, layers), :] = row_ref[0]
    zonal_pad[pl.ds(PAD, layers), :] = last_ref[0]
    for k in range(layers // STEP):
        block = block_of(k)
        thick, diagonals = operator(
            shifted(depth_pad, k),
            row_ref[1, block, :].astype(jnp.int32),
            row_ref[2, block, :],
            row_ref[3, block, :],
            layers_of(k),
            layers,
        )
        zonal = 0.5 * (
            zonal_ref[rows - 1, block, :] + apply_operator(diagonals, shifted(zonal_pad, k))
        )
        zonal_out[block, :] = zonal
        wind = last_ref[0, block, :]
        energy = energy + 0.25 * (
            (last_ref[1, block, :] + row_ref[0, block, :]) * (wind * wind)
            - (last_ref[2, block, :] + thick) * (zonal * zonal)
        )
    return energy


def finish_sums(tracers, sums, energy, sums_out):
    lane = lax.broadcasted_iota(jnp.int32, (STEP, 128), 1)
    energy = jnp.sum(energy, axis=1, keepdims=True)
    row = jnp.sum(jnp.where(lane == tracers, energy, sums), axis=0, keepdims=True)
    sums_out[...] = jnp.broadcast_to(row, sums_out.shape)


def east_first_body(layers, column_ref, edge_ref, sums_ref, merid_out, energy_out):
    energy_out[...] = sums_ref[1] + east_faces(column_ref, edge_ref, layers, merid_out)


def north_last_body(
    tracers,
    row_ref,
    zonal_ref,
    last_ref,
    sums_ref,
    energy_ref,
    zonal_out,
    sums_out,
    depth_pad,
    zonal_pad,
):
    energy = north_faces(
        row_ref, zonal_ref, last_ref, energy_ref[...], zonal_out, depth_pad, zonal_pad
    )
    finish_sums(tracers, sums_ref[0], energy, sums_out)


def east_faces(column_ref, edge_ref, layers, merid_out):
    rows = STEP // 4
    lane = lax.broadcasted_iota(jnp.int32, (STEP, 128), 1)
    sublane = lax.broadcasted_iota(jnp.int32, (STEP, 128), 0)
    packed = column_ref[...]
    edge = edge_ref[...]
    own_thick, own_merid, depth, wind = (
        pltpu.roll(edge, STEP - i * rows, 0) if i else edge for i in range(4)
    )
    thick, diagonals = operator(
        lambda d: pltpu.roll(packed, -d % 128, 1),
        pltpu.roll(packed, STEP - rows, 0).astype(jnp.int32),
        pltpu.roll(packed, STEP - 2 * rows, 0),
        pltpu.roll(packed, STEP - 3 * rows, 0),
        lane,
        layers,
    )
    merid = 0.5 * (
        own_merid + apply_operator(diagonals, lambda d: pltpu.roll(wind, -d % 128, 1))
    )
    merid_out[...] = merid
    kinetic = (depth + packed) * (wind * wind) - (own_thick + thick) * (merid * merid)
    inside = (lane < layers) & (sublane < rows)
    return jnp.where(inside, 0.25 * kinetic, 0.0)


def correct_body(
    gathered_ref,
    tracer_ref,
    warmth_ref,
    zonal_ref,
    last_ref,
    merid_ref,
    edge_ref,
    tracers_out,
    warmth_out,
    zonal_out,
    merid_out,
    new_s,
    heat_s,
    merid_s,
    columns_s,
    sem,
):
    tracers = tracer_ref.shape[0]
    last = zonal_ref.shape[0] - 1
    totals = jnp.sum(gathered_ref[...], axis=0, keepdims=True)
    spread = [
        jnp.broadcast_to(totals[:, i : i + 1], (1, 128)) for i in range(tracers + 2)
    ]
    scale = 1.0 / spread[tracers + 1]
    columns_s[...] = jnp.zeros_like(columns_s)
    copies = []
    for r in range(last + 1):
        source = last_ref if r == last else zonal_ref.at[r]
        copies.append(pltpu.make_async_copy(source, zonal_out.at[r], sem.at[tracers + 1 + r]))
        copies[-1].start()
    for t in range(tracers):
        new_s[t] = tracer_ref[t] + spread[t] * scale
        copies.append(pltpu.make_async_copy(new_s.at[t], tracers_out.at[t], sem.at[t]))
        copies[-1].start()
    columns_s[pl.ds(0, STEP), :] = edge_ref[...]
    across = columns_s[...].T[0 : merid_ref.shape[1]]
    at_edge = lax.broadcasted_iota(jnp.int32, across.shape, 1) == 127
    for r in range(last + 1):
        merid_s[r] = jnp.where(at_edge, pltpu.roll(across, 127 - r, 1), merid_ref[r])
    copies.append(pltpu.make_async_copy(merid_s, merid_out, sem.at[tracers + 2 + last]))
    copies[-1].start()
    heat_s[...] = warmth_ref[...] + spread[tracers] * (scale * (1.0 / HEAT))
    copies.append(pltpu.make_async_copy(heat_s, warmth_out, sem.at[tracers]))
    copies[-1].start()
    for copy in copies:
        copy.wait()


def ring_shift(value, axis, steps):
    count = lax.axis_size(axis)
    return lax.ppermute(value, axis, [(i, (i + steps) % count) for i in range(count)])


def kernel(body, flops, moved, scratch, near, outs, operands):
    operands = [
        pltpu.with_memory_space_constraint(x, pltpu.VMEM if i in near else pltpu.HBM)
        for i, x in enumerate(operands)
    ]
    vmem = pl.BlockSpec(memory_space=pltpu.VMEM)
    hbm = pl.BlockSpec(memory_space=pl.ANY)
    return pl.pallas_call(
        body,
        out_shape=tuple(
            pltpu.VMEM(shape, jnp.float32)
            if place == "vmem"
            else jax.ShapeDtypeStruct(shape, jnp.float32)
            for shape, place in outs
        ),
        in_specs=[vmem] * len(operands),
        out_specs=tuple(hbm if place == "any" else vmem for _, place in outs),
        scratch_shapes=scratch,
        cost_estimate=pl.CostEstimate(flops=flops, bytes_accessed=moved, transcendentals=0),
        compiler_params=pltpu.CompilerParams(vmem_limit_bytes=24 * 2**20),
    )(*operands)


def local(species, zonal, merid, warmth, depth, level, start, end):
    tracers = species.shape[0]
    plane = rows, layers, columns = depth.shape
    devices = lax.axis_size(("gx", "gy"))
    tall = layers + 2 * PAD
    tile = (STEP, 128)
    real = functools.partial(pltpu.VMEM, dtype=jnp.float32)
    row_halo, column_halo = kernel(
        pack_body,
        100_000,
        600_000,
        [real((128, 128))],
        (),
        [((4, layers, columns), "vmem"), (tile, "vmem")],
        (depth, level, start, end),
    )
    column_halo = ring_shift(column_halo, "gx", -1)
    row_halo = ring_shift(row_halo, "gy", -1)
    tracer_new, warmth_new, zonal_part, merid_part, last, edge, parts = kernel(
        own_body,
        20_000_000,
        2_000_000,
        [
            real((rows, tall, columns)),
            real((rows, tall, columns)),
            real((rows, tall, columns)),
            real((rows, tall, columns)),
            real((tracers + 1, rows, tall, columns)),
            real(plane),
            real(plane),
            real((128, 128)),
        ],
        (),
        [
            ((tracers, *plane), "vmem"),
            (plane, "vmem"),
            (plane, "vmem"),
            (plane, "vmem"),
            ((3, layers, columns), "vmem"),
            (tile, "vmem"),
            ((2, *tile), "vmem"),
        ],
        (species, zonal, merid, warmth, depth, level, start, end),
    )
    merid_last, energy = kernel(
        functools.partial(east_first_body, layers),
        200_000,
        200_000,
        [],
        range(3),
        [(tile, "vmem"), (tile, "vmem")],
        (column_halo, edge, parts),
    )
    zonal_last, sums = kernel(
        functools.partial(north_last_body, tracers),
        2_000_000,
        500_000,
        [real((tall, columns)), real((tall, columns))],
        range(5),
        [((layers, columns), "vmem"), ((devices, 128), "vmem")],
        (row_halo, zonal_part, last, parts, energy),
    )
    gathered = lax.all_to_all(sums.reshape(devices, 1, 128), ("gx", "gy"), 0, 0, tiled=True)
    tracers_out, warmth_out, zonal_new, merid_new = kernel(
        correct_body,
        1_000_000,
        2_000_000,
        [
            real((tracers, *plane)),
            real(plane),
            real(plane),
            real((128, 128)),
            pltpu.SemaphoreType.DMA((tracers + 2 + rows,)),
        ],
        range(7),
        [((tracers, *plane), "any"), (plane, "any"), (plane, "any"), (plane, "any")],
        (
            gathered.reshape(devices, 128),
            tracer_new,
            warmth_new,
            zonal_part,
            zonal_last,
            merid_part,
            merid_last,
        ),
    )
    return tracers_out, zonal_new, merid_new, warmth_out


def solution(mesh):
    plane = P("gy", None, "gx")
    stack = P(None, "gy", None, "gx")
    return jax.shard_map(
        local,
        mesh=mesh,
        in_specs=(stack,) + (plane,) * 7,
        out_specs=(stack, plane, plane, plane),
        check_vma=False,
    )
```

time: 42.2 us -> 39.9 us (0.945)
  blocking collectives: 0 us -> 25.5 us
  starting transfers between devices: 18 us -> 6.73 us
  waiting for transfers between devices: 8.56 us -> 0.01 us
  Pallas kernels: 14.9 us -> 6.82 us
    all_to_all x0 -> x1, blocking collectives: none -> 25.5 us  [local(): lax.all_to_all(sums.reshape(devices, 1, 128), ('gx', 'gy'), 0, 0, tiled=T...]
    all_to_all x1 -> x0, starting transfers between devices: 11.2 us -> none  [local(): lax.all_to_all(sums.reshape(devices, 1, 128), ('gx', 'gy'), 0, 0, tiled=T...]
    all_to_all x1 -> x0, waiting for transfers between devices: 8.56 us -> none  [local(): lax.all_to_all(sums.reshape(devices, 1, 128), ('gx', 'gy'), 0, 0, tiled=T...]
    pallas_call x5, Pallas kernels: 14.9 us -> 6.82 us  [kernel(): pl.pallas_call(body, out_shape=tuple((pltpu.VMEM(shape, jnp.float32) if p...]
  transfers between devices with their start and end apart: 3 -> 2, of which waited for: 1 -> 0; matrix products, arithmetic and copies ran while one was open for 0% -> 0% of each run, Pallas kernels for 23% -> 10%
where the time goes in v3:
time: 39.9 us; the launch traced here: 39.8 us
  blocking collectives  25.5 us (64%)
  Pallas kernels  6.82 us (17%)
  starting transfers between devices  6.73 us (17%)
  between operations  0.65 us (2%)
    all_to_all x1, blocking collectives, local(): lax.all_to_all(sums.reshape(devices, 1, 128), ('gx', 'gy'), 0, 0, tiled=T...  25.5 us
    pallas_call x5, Pallas kernels, kernel(): pl.pallas_call(body, out_shape=tuple((pltpu.VMEM(shape, jnp.float32) if p...  6.82 us
    ppermute x2, starting transfers between devices, ring_shift(): lax.ppermute(value, axis, [(i, (i + steps) % count) for i in range(count)])  6.73 us
  transfers between devices with their start and end apart: 2, of which 0 were waited for; matrix products, arithmetic and copies ran while one was open for 0% of the time, Pallas kernels for 10%

profile of v3, /device:TPU:1, one launch (start us, length us, event | category | flops | bytes accessed | tf_op | source)
XLA Modules:
  0.0 39.8 jit_solution(7884235884895466490)
XLA Ops:
  0.6 1.2 %shard_map.111 = (f32[4,120,128]{2,1,0:T(8,128)S(1)}, f32[8,128]{1,0:T(8,128)S(1)}) custom-call(f32[2,120,128]{2,1,0:T(8,128)} %depth_ref.3, s32[2,120,128]{2,1,0:T(8,128)} %level_ref.3, bf16[2,120,128]{2,1,0:T(8,128)(2,1)} %start_ref.3, bf16[2,120,128]{2,1,0:T(8,128)(2,1)} %end_ref.3), custom_call_target="tpu_custom_call" | custom-call | flops 100000 | bytes 600000 | tf_op jit(solution)/shard_map/pallas_call | solution.py:399
  1.8 3.2 %collective-permute-start = (f32[4,120,128]{2,1,0:T(8,128)S(1)}, f32[4,120,128]{2,1,0:T(8,128)S(1)}, u32[]{:S(2)}, u32[]{:S(2)}) collective-permute-start(f32[4,120,128]{2,1,0:T(8,128)S(1)} %get-tuple-element.21), channel_id=1, source_target_pairs={{0,31},{1,0},{2,1},{3,2},{4,3},{5,4},{6,5},{7,6},{8,7},{9,8},{10,9... | collective-permute-start | bytes 737288 | tf_op jit(solution)/shard_map/ppermute | solution.py:389
  5.0 3.5 %collective-permute-start.1 = (f32[8,128]{1,0:T(8,128)S(1)}, f32[8,128]{1,0:T(8,128)S(1)}, u32[]{:S(2)}, u32[]{:S(2)}) collective-permute-start(f32[8,128]{1,0:T(8,128)S(1)} %get-tuple-element.25), channel_id=1, source_target_pairs={{0,224},{32,0},{64,32},{96,64},{128,96},{160,128},{192,160},{224,1... | collective-permute-start | bytes 12296 | tf_op jit(solution)/shard_map/ppermute | solution.py:389
  8.5 3.8 %shard_map.112 = (f32[8,2,120,128]{3,2,1,0:T(8,128)S(1)}, f32[2,120,128]{2,1,0:T(8,128)S(1)}, f32[2,120,128]{2,1,0:T(8,128)S(1)}, f32[2,120,128]{2,1,0:T(8,128)S...) custom-call(bf16[8,2,120,128]{3,2,1,0:T(8,128)(2,1)} %species_ref.1, ...), custom_call_target="tpu_custom_call" | custom-call | flops 20000000 | bytes 2000000 | tf_op jit(solution)/shard_map/pallas_call | solution.py:399
  12.3 0.0 collective-permute-done.1.column_ref
  12.3 0.1 shard_map.113
  12.4 0.0 collective-permute-done.row_ref
  12.4 0.4 %shard_map.114 = (f32[120,128]{1,0:T(8,128)S(1)}, f32[256,128]{1,0:T(8,128)S(1)}) custom-call(f32[4,120,128]{2,1,0:T(8,128)S(1)} %collective-permute-done.row_ref, f32[2,120,128]{2,1,0:T(8,128)S(1)} %get-tuple-element.22.zonal_ref, f32[3,120,128]{2,1,0:T(8,128)S(1)} %get-tuple-element.23.last_ref, f32[2,8,128]{2,1,0:T(8,128)S(1)} %get-tuple-element.24.sums_ref, ...), custom_call_target="tpu_custom_call" | custom-call | flops 2000000 | bytes 500000 | tf_op jit(solution)/shard_map/pallas_call | solution.py:399
  12.9 25.5 %all_to_all.5 = f32[256,1,128]{2,1,0:T(1,128)S(1)} all-to-all(f32[256,1,128]{2,1,0:T(1,128)S(1)} %bitcast.5), channel_id=1, replica_groups=mesh['gx'=8,'gy'=32] {'gx','gy'}, dimensions={0} | all-to-all | bytes 262144 | tf_op jit(solution)/shard_map/all_to_all | solution.py:477
  38.4 1.3 %shard_map.115 = (f32[8,2,120,128]{3,2,1,0:T(8,128)}, f32[2,120,128]{2,1,0:T(8,128)}, f32[2,120,128]{2,1,0:T(8,128)}, f32[2,120,128]{2,1,0:T(8,128)}) custom-call(f32[256,128]{1,0:T(8,128)S(1)} %bitcast.4, f32[8,2,120,128]{3,2,1,0:T(8,128)S(1)} %get-tuple-element.29.tracer_ref, f32[2,120,128]{2,1,0:T(8,128)S(1)} %get-tuple-element.30.warmth_ref, ...), custom_call_target="tpu_custom_call" | custom-call | flops 1000000 | bytes 2000000 | tf_op jit(solution)/shard_map/pallas_call | solution.py:399
Async XLA Ops:
  1.8 10.6 %collective-permute-start = (f32[4,120,128]{2,1,0:T(8,128)S(1)}, f32[4,120,128]{2,1,0:T(8,128)S(1)}, u32[]{:S(2)}, u32[]{:S(2)}) collective-permute-start(f32[4,120,128]{2,1,0:T(8,128)S(1)} %get-tuple-element.21), channel_id=1, source_target_pairs={{0,31},{1,0},{2,1},{3,2},{4,3},{5,4},{6,5},{7,6},{8,7},{9,8},{10,9... | collective-permute-start | bytes 737288 | tf_op jit(solution)/shard_map/ppermute | solution.py:389
  5.0 7.3 %collective-permute-start.1 = (f32[8,128]{1,0:T(8,128)S(1)}, f32[8,128]{1,0:T(8,128)S(1)}, u32[]{:S(2)}, u32[]{:S(2)}) collective-permute-start(f32[8,128]{1,0:T(8,128)S(1)} %get-tuple-element.25), channel_id=1, source_target_pairs={{0,224},{32,0},{64,32},{96,64},{128,96},{160,128},{192,160},{224,1... | collective-permute-start | bytes 12296 | tf_op jit(solution)/shard_map/ppermute | solution.py:389

commit v4 on v3

--- a/solution.py
+++ b/solution.py
@@ -5,8 +5,15 @@
 from jax import lax
 from jax.experimental import pallas as pl
 from jax.experimental.pallas import tpu as pltpu
+from jax.sharding import Mesh
 from jax.sharding import PartitionSpec as P
 
+
+SPLIT = (4, 2, 2, 4, 2, 2)
+NAMES = ("y", "x_hi", "z_hi", "z_lo", "x_lo", "core")
+GX = NAMES[:2]
+GY = NAMES[2:]
+CUBE = ("y", "x_hi", "z_lo", "x_lo")
 
 HEAT = 3.5
 PAD = 8
@@ -283,8 +290,7 @@
 def finish_sums(tracers, sums, energy, sums_out):
     lane = lax.broadcasted_iota(jnp.int32, (STEP, 128), 1)
     energy = jnp.sum(energy, axis=1, keepdims=True)
-    row = jnp.sum(jnp.where(lane == tracers, energy, sums), axis=0, keepdims=True)
-    sums_out[...] = jnp.broadcast_to(row, sums_out.shape)
+    sums_out[...] = jnp.sum(jnp.where(lane == tracers, energy, sums), axis=0, keepdims=True)
 
 
 def east_first_body(layers, column_ref, edge_ref, sums_ref, merid_out, energy_out):
@@ -389,6 +395,18 @@
     return lax.ppermute(value, axis, [(i, (i + steps) % count) for i in range(count)])
 
 
+def add_mirrored(value, axis):
+    count = lax.axis_size(axis)
+    return value + lax.ppermute(value, axis, [(i, count - 1 - i) for i in range(count)])
+
+
+def sums_to_gather(sums):
+    sums = add_mirrored(add_mirrored(sums, "core"), ("z_hi", "z_lo"))
+    count = lax.axis_size(CUBE)
+    rows = jnp.broadcast_to(sums[None], (count, *sums.shape))
+    return lax.all_to_all(rows, CUBE, 0, 0, tiled=True).reshape(count, 128)
+
+
 def kernel(body, flops, moved, scratch, near, outs, operands):
     operands = [
         pltpu.with_memory_space_constraint(x, pltpu.VMEM if i in near else pltpu.HBM)
@@ -415,7 +433,6 @@
 def local(species, zonal, merid, warmth, depth, level, start, end):
     tracers = species.shape[0]
     plane = rows, layers, columns = depth.shape
-    devices = lax.axis_size(("gx", "gy"))
     tall = layers + 2 * PAD
     tile = (STEP, 128)
     real = functools.partial(pltpu.VMEM, dtype=jnp.float32)
@@ -428,8 +445,8 @@
         [((4, layers, columns), "vmem"), (tile, "vmem")],
         (depth, level, start, end),
     )
-    column_halo = ring_shift(column_halo, "gx", -1)
-    row_halo = ring_shift(row_halo, "gy", -1)
+    column_halo = ring_shift(column_halo, GX, -1)
+    row_halo = ring_shift(row_halo, GY, -1)
     tracer_new, warmth_new, zonal_part, merid_part, last, edge, parts = kernel(
         own_body,
         20_000_000,
@@ -471,10 +488,10 @@
         500_000,
         [real((tall, columns)), real((tall, columns))],
         range(5),
-        [((layers, columns), "vmem"), ((devices, 128), "vmem")],
+        [((layers, columns), "vmem"), ((1, 128), "vmem")],
         (row_halo, zonal_part, last, parts, energy),
     )
-    gathered = lax.all_to_all(sums.reshape(devices, 1, 128), ("gx", "gy"), 0, 0, tiled=True)
+    gathered = sums_to_gather(sums)
     tracers_out, warmth_out, zonal_new, merid_new = kernel(
         correct_body,
         1_000_000,
@@ -489,7 +506,7 @@
         range(7),
         [((tracers, *plane), "any"), (plane, "any"), (plane, "any"), (plane, "any")],
         (
-            gathered.reshape(devices, 128),
+            gathered,
             tracer_new,
             warmth_new,
             zonal_part,
@@ -502,11 +519,12 @@
 
 
 def solution(mesh):
-    plane = P("gy", None, "gx")
-    stack = P(None, "gy", None, "gx")
+    split = Mesh(mesh.devices.reshape(SPLIT), NAMES)
+    plane = P(GY, None, GX)
+    stack = P(None, GY, None, GX)
     return jax.shard_map(
         local,
-        mesh=mesh,
+        mesh=split,
         in_specs=(stack,) + (plane,) * 7,
         out_specs=(stack, plane, plane, plane),
         check_vma=False,

time: 39.9 us -> 39.7 us (level); the launches traced: 39.8 us -> 39 us
  blocking collectives: 25.5 us -> 14.1 us
  starting transfers between devices: 6.73 us -> 13.7 us
  waiting for transfers between devices: 0.01 us -> 3.73 us
    all_to_all x1, blocking collectives: 25.5 us -> 14.1 us  [sums_to_gather(): return lax.all_to_all(rows, CUBE, 0, 0, tiled=True).reshape(count, 128)]
    ppermute x0 -> x2, starting transfers between devices: none -> 6.94 us  [add_mirrored(): lax.ppermute(value, axis, [(i, count - 1 - i) for i in range(count)])]
    ppermute x0 -> x2, waiting for transfers between devices: none -> 3.72 us  [add_mirrored(): lax.ppermute(value, axis, [(i, count - 1 - i) for i in range(count)])]
  transfers between devices with their start and end apart: 2 -> 4, of which waited for: 0 -> 2; matrix products, arithmetic and copies ran while one was open for 0% -> 0% of each run, Pallas kernels for 10% -> 10%
where the time goes in v4:
time: 39.7 us; the launch traced here: 39 us
  blocking collectives  14.1 us (36%)
  starting transfers between devices  13.7 us (35%)
  Pallas kernels  6.76 us (17%)
  waiting for transfers between devices  3.73 us (9%)
  between operations  0.66 us (2%)
    all_to_all x1, blocking collectives, sums_to_gather(): return lax.all_to_all(rows, CUBE, 0, 0, tiled=True).reshape(count, 128)  14.1 us
    ppermute x2, starting transfers between devices, add_mirrored(): lax.ppermute(value, axis, [(i, count - 1 - i) for i in range(count)])  6.94 us
    pallas_call x5, Pallas kernels, kernel(): pl.pallas_call(body, out_shape=tuple((pltpu.VMEM(shape, jnp.float32) if p...  6.76 us
    ppermute x2, starting transfers between devices, ring_shift(): lax.ppermute(value, axis, [(i, (i + steps) % count) for i in range(count)])  6.73 us
    ppermute x2, waiting for transfers between devices, add_mirrored(): lax.ppermute(value, axis, [(i, count - 1 - i) for i in range(count)])  3.72 us
  transfers between devices with their start and end apart: 4, of which 2 were waited for; matrix products, arithmetic and copies ran while one was open for 0% of the time, Pallas kernels for 10%

profile of v4, /device:TPU:1, one launch (start us, length us, event | category | flops | bytes accessed | tf_op | source)
XLA Modules:
  0.0 39.0 jit_solution(1722722423496726948)
XLA Ops:
  0.6 1.2 %shard_map.111 = (f32[4,120,128]{2,1,0:T(8,128)S(1)}, f32[8,128]{1,0:T(8,128)S(1)}) custom-call(f32[2,120,128]{2,1,0:T(8,128)} %depth_ref.3, s32[2,120,128]{2,1,0:T(8,128)} %level_ref.3, bf16[2,120,128]{2,1,0:T(8,128)(2,1)} %start_ref.3, bf16[2,120,128]{2,1,0:T(8,128)(2,1)} %end_ref.3), custom_call_target="tpu_custom_call" | custom-call | flops 100000 | bytes 600000 | tf_op jit(solution)/shard_map/pallas_call | solution.py:417
  1.8 3.2 %collective-permute-start = (f32[4,120,128]{2,1,0:T(8,128)S(1)}, f32[4,120,128]{2,1,0:T(8,128)S(1)}, u32[]{:S(2)}, u32[]{:S(2)}) collective-permute-start(f32[4,120,128]{2,1,0:T(8,128)S(1)} %get-tuple-element.21), channel_id=1, source_target_pairs={{0,31},{1,0},{2,1},{3,2},{4,3},{5,4},{6,5},{7,6},{8,7},{9,8},{10,9... | collective-permute-start | bytes 737288 | tf_op jit(solution)/shard_map/ppermute | solution.py:395
  5.0 3.5 %collective-permute-start.1 = (f32[8,128]{1,0:T(8,128)S(1)}, f32[8,128]{1,0:T(8,128)S(1)}, u32[]{:S(2)}, u32[]{:S(2)}) collective-permute-start(f32[8,128]{1,0:T(8,128)S(1)} %get-tuple-element.25), channel_id=1, source_target_pairs={{0,224},{32,0},{64,32},{96,64},{128,96},{160,128},{192,160},{224,1... | collective-permute-start | bytes 12296 | tf_op jit(solution)/shard_map/ppermute | solution.py:395
  8.5 3.8 %shard_map.112 = (f32[8,2,120,128]{3,2,1,0:T(8,128)S(1)}, f32[2,120,128]{2,1,0:T(8,128)S(1)}, f32[2,120,128]{2,1,0:T(8,128)S(1)}, f32[2,120,128]{2,1,0:T(8,128)S...) custom-call(bf16[8,2,120,128]{3,2,1,0:T(8,128)(2,1)} %species_ref.1, ...), custom_call_target="tpu_custom_call" | custom-call | flops 20000000 | bytes 2000000 | tf_op jit(solution)/shard_map/pallas_call | solution.py:417
  12.3 0.0 collective-permute-done.1.column_ref
  12.3 0.1 shard_map.113
  12.4 0.0 collective-permute-done.row_ref
  12.4 0.4 %shard_map.114 = (f32[120,128]{1,0:T(8,128)S(1)}, f32[1,128]{1,0:T(1,128)S(1)}) custom-call(f32[4,120,128]{2,1,0:T(8,128)S(1)} %collective-permute-done.row_ref, f32[2,120,128]{2,1,0:T(8,128)S(1)} %get-tuple-element.22.zonal_ref, f32[3,120,128]{2,1,0:T(8,128)S(1)} %get-tuple-element.23.last_ref, f32[2,8,128]{2,1,0:T(8,128)S(1)} %get-tuple-element.24.sums_ref, ...), custom_call_target="tpu_custom_call" | custom-call | flops 2000000 | bytes 500000 | tf_op jit(solution)/shard_map/pallas_call | solution.py:417
  12.8 6.2 %collective-permute-start.2 = (f32[1,128]{1,0:T(1,128)S(1)}, f32[1,128]{1,0:T(1,128)S(1)}, u32[]{:S(2)}, u32[]{:S(2)}) collective-permute-start(f32[1,128]{1,0:T(1,128)S(1)} %get-tuple-element.28), channel_id=1, source_target_pairs={{0,1},{1,0},{2,3},{3,2},{4,5},{5,4},{6,7},{7,6},{8,9},{9,8},{10,11... | collective-permute-start | bytes 1544 | tf_op jit(solution)/shard_map/ppermute | solution.py:400
  19.1 0.8 %collective-permute-done.2 = f32[1,128]{1,0:T(1,128)S(1)} collective-permute-done((f32[1,128]{1,0:T(1,128)S(1)}, f32[1,128]{1,0:T(1,128)S(1)}, u32[]{:S(2)}, u32[]{:S(2)}) %collective-permute-start.2) | collective-permute-done | bytes 544 | tf_op jit(solution)/shard_map/ppermute | solution.py:400
  19.9 0.7 %collective-permute-start.3 = (f32[1,128]{1,0:T(1,128)S(1)}, f32[1,128]{1,0:T(1,128)S(1)}, u32[]{:S(2)}, u32[]{:S(2)}) collective-permute-start(f32[1,128]{1,0:T(1,128)S(1)} %add.6), channel_id=1, source_target_pairs={{0,28},{4,24},{8,20},{12,16},{16,12},{20,8},{24,4},{28,0},{1,29},{... | collective-permute-start | bytes 1544 | tf_op jit(solution)/shard_map/ppermute | solution.py:400
  20.6 2.9 %collective-permute-done.3 = f32[1,128]{1,0:T(1,128)S(1)} collective-permute-done((f32[1,128]{1,0:T(1,128)S(1)}, f32[1,128]{1,0:T(1,128)S(1)}, u32[]{:S(2)}, u32[]{:S(2)}) %collective-permute-start.3) | collective-permute-done | bytes 544 | tf_op jit(solution)/shard_map/ppermute | solution.py:400
  23.6 14.1 %all_to_all.5 = f32[64,1,128]{2,1,0:T(1,128)S(1)} all-to-all(f32[64,1,128]{2,1,0:T(1,128)S(1)} %broadcast_in_dim.9), channel_id=1, replica_groups=mesh['y'=4,'x_hi'=2,'z_hi'=2,'z_lo'=4,'x_lo'=2,'core'=2] {'y','x_hi','z_..., dimensions={0} | all-to-all | bytes 65536 | tf_op jit(solution)/shard_map/all_to_all | solution.py:407
  37.7 1.3 %shard_map.115 = (f32[8,2,120,128]{3,2,1,0:T(8,128)}, f32[2,120,128]{2,1,0:T(8,128)}, f32[2,120,128]{2,1,0:T(8,128)}, f32[2,120,128]{2,1,0:T(8,128)}) custom-call(f32[64,128]{1,0:T(8,128)S(1)} %bitcast.3, f32[8,2,120,128]{3,2,1,0:T(8,128)S(1)} %get-tuple-element.29.tracer_ref, f32[2,120,128]{2,1,0:T(8,128)S(1)} %get-tuple-element.30.warmth_ref, ...), custom_call_target="tpu_custom_call" | custom-call | flops 1000000 | bytes 2000000 | tf_op jit(solution)/shard_map/pallas_call | solution.py:417
  (3 shorter events, 0.0 us)
Async XLA Ops:
  1.8 10.6 %collective-permute-start = (f32[4,120,128]{2,1,0:T(8,128)S(1)}, f32[4,120,128]{2,1,0:T(8,128)S(1)}, u32[]{:S(2)}, u32[]{:S(2)}) collective-permute-start(f32[4,120,128]{2,1,0:T(8,128)S(1)} %get-tuple-element.21), channel_id=1, source_target_pairs={{0,31},{1,0},{2,1},{3,2},{4,3},{5,4},{6,5},{7,6},{8,7},{9,8},{10,9... | collective-permute-start | bytes 737288 | tf_op jit(solution)/shard_map/ppermute | solution.py:395
  5.0 7.3 %collective-permute-start.1 = (f32[8,128]{1,0:T(8,128)S(1)}, f32[8,128]{1,0:T(8,128)S(1)}, u32[]{:S(2)}, u32[]{:S(2)}) collective-permute-start(f32[8,128]{1,0:T(8,128)S(1)} %get-tuple-element.25), channel_id=1, source_target_pairs={{0,224},{32,0},{64,32},{96,64},{128,96},{160,128},{192,160},{224,1... | collective-permute-start | bytes 12296 | tf_op jit(solution)/shard_map/ppermute | solution.py:395
  12.8 7.0 %collective-permute-start.2 = (f32[1,128]{1,0:T(1,128)S(1)}, f32[1,128]{1,0:T(1,128)S(1)}, u32[]{:S(2)}, u32[]{:S(2)}) collective-permute-start(f32[1,128]{1,0:T(1,128)S(1)} %get-tuple-element.28), channel_id=1, source_target_pairs={{0,1},{1,0},{2,3},{3,2},{4,5},{5,4},{6,7},{7,6},{8,9},{9,8},{10,11... | collective-permute-start | bytes 1544 | tf_op jit(solution)/shard_map/ppermute | solution.py:400
  19.9 3.6 %collective-permute-start.3 = (f32[1,128]{1,0:T(1,128)S(1)}, f32[1,128]{1,0:T(1,128)S(1)}, u32[]{:S(2)}, u32[]{:S(2)}) collective-permute-start(f32[1,128]{1,0:T(1,128)S(1)} %add.6), channel_id=1, source_target_pairs={{0,28},{4,24},{8,20},{12,16},{16,12},{20,8},{24,4},{28,0},{1,29},{... | collective-permute-start | bytes 1544 | tf_op jit(solution)/shard_map/ppermute | solution.py:400

commit v5 on v4

--- a/solution.py
+++ b/solution.py
@@ -341,48 +341,39 @@
     return jnp.where(inside, 0.25 * kinetic, 0.0)
 
 
-def correct_body(
-    gathered_ref,
-    tracer_ref,
-    warmth_ref,
-    zonal_ref,
-    last_ref,
-    merid_ref,
-    edge_ref,
-    tracers_out,
-    warmth_out,
-    zonal_out,
-    merid_out,
-    new_s,
-    heat_s,
-    merid_s,
-    columns_s,
-    sem,
+def winds_body(
+    zonal_ref, last_ref, merid_ref, edge_ref, zonal_out, merid_out, merid_s, columns_s, sem
 ):
+    rows, layers, _ = merid_ref.shape
+    copies = []
+    for r in range(rows):
+        source = last_ref if r + 1 == rows else zonal_ref.at[r]
+        copies.append(pltpu.make_async_copy(source, zonal_out.at[r], sem.at[r]))
+        copies[-1].start()
+    columns_s[...] = jnp.zeros_like(columns_s)
+    columns_s[pl.ds(0, STEP), :] = edge_ref[...]
+    across = columns_s[...].T[0:layers]
+    at_edge = lax.broadcasted_iota(jnp.int32, across.shape, 1) == 127
+    for r in range(rows):
+        merid_s[r] = jnp.where(at_edge, pltpu.roll(across, 127 - r, 1), merid_ref[r])
+    copies.append(pltpu.make_async_copy(merid_s, merid_out, sem.at[rows]))
+    copies[-1].start()
+    for copy in copies:
+        copy.wait()
+
+
+def correct_body(gathered_ref, tracer_ref, warmth_ref, tracers_out, warmth_out, new_s, heat_s, sem):
     tracers = tracer_ref.shape[0]
-    last = zonal_ref.shape[0] - 1
     totals = jnp.sum(gathered_ref[...], axis=0, keepdims=True)
     spread = [
         jnp.broadcast_to(totals[:, i : i + 1], (1, 128)) for i in range(tracers + 2)
     ]
     scale = 1.0 / spread[tracers + 1]
-    columns_s[...] = jnp.zeros_like(columns_s)
     copies = []
-    for r in range(last + 1):
-        source = last_ref if r == last else zonal_ref.at[r]
-        copies.append(pltpu.make_async_copy(source, zonal_out.at[r], sem.at[tracers + 1 + r]))
-        copies[-1].start()
     for t in range(tracers):
         new_s[t] = tracer_ref[t] + spread[t] * scale
         copies.append(pltpu.make_async_copy(new_s.at[t], tracers_out.at[t], sem.at[t]))
         copies[-1].start()
-    columns_s[pl.ds(0, STEP), :] = edge_ref[...]
-    across = columns_s[...].T[0 : merid_ref.shape[1]]
-    at_edge = lax.broadcasted_iota(jnp.int32, across.shape, 1) == 127
-    for r in range(last + 1):
-        merid_s[r] = jnp.where(at_edge, pltpu.roll(across, 127 - r, 1), merid_ref[r])
-    copies.append(pltpu.make_async_copy(merid_s, merid_out, sem.at[tracers + 2 + last]))
-    copies[-1].start()
     heat_s[...] = warmth_ref[...] + spread[tracers] * (scale * (1.0 / HEAT))
     copies.append(pltpu.make_async_copy(heat_s, warmth_out, sem.at[tracers]))
     copies[-1].start()
@@ -401,7 +392,8 @@
 
 
 def sums_to_gather(sums):
-    sums = add_mirrored(add_mirrored(sums, "core"), ("z_hi", "z_lo"))
+    sums = add_mirrored(sums, "core")
+    sums = add_mirrored(sums, ("z_hi", "z_lo"))
     count = lax.axis_size(CUBE)
     rows = jnp.broadcast_to(sums[None], (count, *sums.shape))
     return lax.all_to_all(rows, CUBE, 0, 0, tiled=True).reshape(count, 128)
@@ -492,28 +484,23 @@
         (row_halo, zonal_part, last, parts, energy),
     )
     gathered = sums_to_gather(sums)
-    tracers_out, warmth_out, zonal_new, merid_new = kernel(
+    zonal_new, merid_new = kernel(
+        winds_body,
+        200_000,
+        700_000,
+        [real(plane), real((128, 128)), pltpu.SemaphoreType.DMA((rows + 1,))],
+        range(4),
+        [(plane, "any"), (plane, "any")],
+        (zonal_part, zonal_last, merid_part, merid_last),
+    )
+    tracers_out, warmth_out = kernel(
         correct_body,
         1_000_000,
         2_000_000,
-        [
-            real((tracers, *plane)),
-            real(plane),
-            real(plane),
-            real((128, 128)),
-            pltpu.SemaphoreType.DMA((tracers + 2 + rows,)),
-        ],
-        range(7),
-        [((tracers, *plane), "any"), (plane, "any"), (plane, "any"), (plane, "any")],
-        (
-            gathered,
-            tracer_new,
-            warmth_new,
-            zonal_part,
-            zonal_last,
-            merid_part,
-            merid_last,
-        ),
+        [real((tracers, *plane)), real(plane), pltpu.SemaphoreType.DMA((tracers + 1,))],
+        range(3),
+        [((tracers, *plane), "any"), (plane, "any")],
+        (gathered, tracer_new, warmth_new),
     )
     return tracers_out, zonal_new, merid_new, warmth_out
 

time: 39.7 us -> 40.3 us (1.015)
  blocking collectives: 14.1 us -> 0 us
  waiting for transfers between devices: 3.73 us -> 11.7 us
  starting transfers between devices: 13.7 us -> 19.1 us
  Pallas kernels: 6.76 us -> 7.51 us
  local copies, waits for them, and re-layouts: 0.02 us -> 0.64 us
    all_to_all x1 -> x0, blocking collectives: 14.1 us -> none  [sums_to_gather(): return lax.all_to_all(rows, CUBE, 0, 0, tiled=True).reshape(count, 128)]
    all_to_all x0 -> x1, waiting for transfers between devices: none -> 7.96 us  [sums_to_gather(): return lax.all_to_all(rows, CUBE, 0, 0, tiled=True).reshape(count, 128)]
    all_to_all x0 -> x1, starting transfers between devices: none -> 5.43 us  [sums_to_gather(): return lax.all_to_all(rows, CUBE, 0, 0, tiled=True).reshape(count, 128)]
    pallas_call x5 -> x6, Pallas kernels: 6.76 us -> 7.51 us  [kernel(): pl.pallas_call(body, out_shape=tuple((pltpu.VMEM(shape, jnp.float32) if p...]
    broadcast_in_dim x1, local copies, waits for them, and re-layouts: 0.02 us -> 0.64 us  [sums_to_gather(): rows = jnp.broadcast_to(sums[None], (count, *sums.shape))]
  transfers between devices with their start and end apart: 4 -> 5, of which waited for: 2 -> 3; matrix products, arithmetic and copies ran while one was open for 0% -> 0% of each run, Pallas kernels for 10% -> 12%
where the time goes in v5:
time: 40.3 us; the launch traced here: 39.6 us
  starting transfers between devices  19.1 us (47%)
  waiting for transfers between devices  11.7 us (29%)
  Pallas kernels  7.51 us (19%)
  between operations  0.67 us (2%)
  local copies, waits for them, and re-layouts  0.64 us (2%)
    all_to_all x1, waiting for transfers between devices, sums_to_gather(): return lax.all_to_all(rows, CUBE, 0, 0, tiled=True).reshape(count, 128)  7.96 us
    pallas_call x6, Pallas kernels, kernel(): pl.pallas_call(body, out_shape=tuple((pltpu.VMEM(shape, jnp.float32) if p...  7.51 us
    ppermute x2, starting transfers between devices, add_mirrored(): lax.ppermute(value, axis, [(i, count - 1 - i) for i in range(count)])  6.94 us
    ppermute x2, starting transfers between devices, ring_shift(): lax.ppermute(value, axis, [(i, (i + steps) % count) for i in range(count)])  6.73 us
    all_to_all x1, starting transfers between devices, sums_to_gather(): return lax.all_to_all(rows, CUBE, 0, 0, tiled=True).reshape(count, 128)  5.43 us
    ppermute x2, waiting for transfers between devices, add_mirrored(): lax.ppermute(value, axis, [(i, count - 1 - i) for i in range(count)])  3.72 us
  transfers between devices with their start and end apart: 5, of which 3 were waited for; matrix products, arithmetic and copies ran while one was open for 0% of the time, Pallas kernels for 12%

profile of v5, /device:TPU:1, one launch (start us, length us, event | category | flops | bytes accessed | tf_op | source)
XLA Modules:
  0.0 39.6 jit_solution(5542985162010689946)
XLA Ops:
  0.6 1.2 %shard_map.111 = (f32[4,120,128]{2,1,0:T(8,128)S(1)}, f32[8,128]{1,0:T(8,128)S(1)}) custom-call(f32[2,120,128]{2,1,0:T(8,128)} %depth_ref.3, s32[2,120,128]{2,1,0:T(8,128)} %level_ref.3, bf16[2,120,128]{2,1,0:T(8,128)(2,1)} %start_ref.3, bf16[2,120,128]{2,1,0:T(8,128)(2,1)} %end_ref.3), custom_call_target="tpu_custom_call" | custom-call | flops 100000 | bytes 600000 | tf_op jit(solution)/shard_map/pallas_call | solution.py:409
  1.8 3.2 %collective-permute-start = (f32[4,120,128]{2,1,0:T(8,128)S(1)}, f32[4,120,128]{2,1,0:T(8,128)S(1)}, u32[]{:S(2)}, u32[]{:S(2)}) collective-permute-start(f32[4,120,128]{2,1,0:T(8,128)S(1)} %get-tuple-element.21), channel_id=1, source_target_pairs={{0,31},{1,0},{2,1},{3,2},{4,3},{5,4},{6,5},{7,6},{8,7},{9,8},{10,9... | collective-permute-start | bytes 737288 | tf_op jit(solution)/shard_map/ppermute | solution.py:386
  5.0 3.5 %collective-permute-start.1 = (f32[8,128]{1,0:T(8,128)S(1)}, f32[8,128]{1,0:T(8,128)S(1)}, u32[]{:S(2)}, u32[]{:S(2)}) collective-permute-start(f32[8,128]{1,0:T(8,128)S(1)} %get-tuple-element.25), channel_id=1, source_target_pairs={{0,224},{32,0},{64,32},{96,64},{128,96},{160,128},{192,160},{224,1... | collective-permute-start | bytes 12296 | tf_op jit(solution)/shard_map/ppermute | solution.py:386
  8.5 3.8 %shard_map.112 = (f32[8,2,120,128]{3,2,1,0:T(8,128)S(1)}, f32[2,120,128]{2,1,0:T(8,128)S(1)}, f32[2,120,128]{2,1,0:T(8,128)S(1)}, f32[2,120,128]{2,1,0:T(8,128)S...) custom-call(bf16[8,2,120,128]{3,2,1,0:T(8,128)(2,1)} %species_ref.1, ...), custom_call_target="tpu_custom_call" | custom-call | flops 20000000 | bytes 2000000 | tf_op jit(solution)/shard_map/pallas_call | solution.py:409
  12.3 0.0 collective-permute-done.1.column_ref
  12.3 0.1 shard_map.113
  12.4 0.0 collective-permute-done.row_ref
  12.4 0.4 %shard_map.114 = (f32[120,128]{1,0:T(8,128)S(1)}, f32[1,128]{1,0:T(1,128)S(1)}) custom-call(f32[4,120,128]{2,1,0:T(8,128)S(1)} %collective-permute-done.row_ref, f32[2,120,128]{2,1,0:T(8,128)S(1)} %get-tuple-element.22.zonal_ref, f32[3,120,128]{2,1,0:T(8,128)S(1)} %get-tuple-element.23.last_ref, f32[2,8,128]{2,1,0:T(8,128)S(1)} %get-tuple-element.24.sums_ref, ...), custom_call_target="tpu_custom_call" | custom-call | flops 2000000 | bytes 500000 | tf_op jit(solution)/shard_map/pallas_call | solution.py:409
  12.8 6.2 %collective-permute-start.2 = (f32[1,128]{1,0:T(1,128)S(1)}, f32[1,128]{1,0:T(1,128)S(1)}, u32[]{:S(2)}, u32[]{:S(2)}) collective-permute-start(f32[1,128]{1,0:T(1,128)S(1)} %get-tuple-element.28), channel_id=1, source_target_pairs={{0,1},{1,0},{2,3},{3,2},{4,5},{5,4},{6,7},{7,6},{8,9},{9,8},{10,11... | collective-permute-start | bytes 1544 | tf_op jit(solution)/shard_map/ppermute | solution.py:391
  19.1 0.8 %collective-permute-done.2 = f32[1,128]{1,0:T(1,128)S(1)} collective-permute-done((f32[1,128]{1,0:T(1,128)S(1)}, f32[1,128]{1,0:T(1,128)S(1)}, u32[]{:S(2)}, u32[]{:S(2)}) %collective-permute-start.2) | collective-permute-done | bytes 544 | tf_op jit(solution)/shard_map/ppermute | solution.py:391
  19.9 0.7 %collective-permute-start.3 = (f32[1,128]{1,0:T(1,128)S(1)}, f32[1,128]{1,0:T(1,128)S(1)}, u32[]{:S(2)}, u32[]{:S(2)}) collective-permute-start(f32[1,128]{1,0:T(1,128)S(1)} %add.6), channel_id=1, source_target_pairs={{0,28},{4,24},{8,20},{12,16},{16,12},{20,8},{24,4},{28,0},{1,29},{... | collective-permute-start | bytes 1544 | tf_op jit(solution)/shard_map/ppermute | solution.py:391
  20.6 2.9 %collective-permute-done.3 = f32[1,128]{1,0:T(1,128)S(1)} collective-permute-done((f32[1,128]{1,0:T(1,128)S(1)}, f32[1,128]{1,0:T(1,128)S(1)}, u32[]{:S(2)}, u32[]{:S(2)}) %collective-permute-start.3) | collective-permute-done | bytes 544 | tf_op jit(solution)/shard_map/ppermute | solution.py:391
  23.5 0.6 %broadcast_in_dim.9 = f32[64,1,128]{2,1,0:T(1,128)} broadcast(f32[128]{0:T(128)S(1)} %add_bitcast_fusion), dimensions={2} | broadcast | bytes 33280 | tf_op jit(solution)/shard_map/broadcast_in_dim | solution.py:398
  24.2 5.4 %all-to-all-start = ((f32[64,1,128]{2,1,0:T(1,128)}), f32[64,1,128]{2,1,0:T(1,128)S(1)}, u32[]{:S(2)}, u32[]{:S(2)}) async-start(f32[64,1,128]{2,1,0:T(1,128)} %broadcast_in_dim.9), calls=%async_computation | async-start | bytes 65536 | tf_op jit(solution)/shard_map/all_to_all | solution.py:399
  29.6 0.9 %shard_map.116 = (f32[2,120,128]{2,1,0:T(8,128)}, f32[2,120,128]{2,1,0:T(8,128)}) custom-call(f32[2,120,128]{2,1,0:T(8,128)S(1)} %get-tuple-element.22.zonal_ref, f32[120,128]{1,0:T(8,128)S(1)} %get-tuple-element.32.last_ref, f32[2,120,128]{2,1,0:T(8,128)S(1)} %get-tuple-element.33.merid_ref, f32[8,128]{1,0:T(8,128)S(1)} %get-tuple-element.34.edge_ref), custom_call_target="tpu_custom_call" | custom-call | flops 200000 | bytes 700000 | tf_op jit(solution)/shard_map/pallas_call | solution.py:409
  30.5 8.0 %all-to-all-done = f32[64,1,128]{2,1,0:T(1,128)S(1)} async-done(((f32[64,1,128]{2,1,0:T(1,128)}), f32[64,1,128]{2,1,0:T(1,128)S(1)}, u32[]{:S(2)}, u32[]{:S(2)}) %all-to-all-start) | async-done | bytes 32800 | tf_op jit(solution)/shard_map/all_to_all | solution.py:399
  38.4 1.2 %shard_map.115 = (f32[8,2,120,128]{3,2,1,0:T(8,128)}, f32[2,120,128]{2,1,0:T(8,128)}) custom-call(f32[64,128]{1,0:T(8,128)S(1)} %bitcast.3, f32[8,2,120,128]{3,2,1,0:T(8,128)S(1)} %get-tuple-element.29.tracer_ref, f32[2,120,128]{2,1,0:T(8,128)S(1)} %get-tuple-element.30.warmth_ref), custom_call_target="tpu_custom_call" | custom-call | flops 1000000 | bytes 2000000 | tf_op jit(solution)/shard_map/pallas_call | solution.py:409
  (2 shorter events, 0.0 us)
Async XLA Ops:
  1.8 10.6 %collective-permute-start = (f32[4,120,128]{2,1,0:T(8,128)S(1)}, f32[4,120,128]{2,1,0:T(8,128)S(1)}, u32[]{:S(2)}, u32[]{:S(2)}) collective-permute-start(f32[4,120,128]{2,1,0:T(8,128)S(1)} %get-tuple-element.21), channel_id=1, source_target_pairs={{0,31},{1,0},{2,1},{3,2},{4,3},{5,4},{6,5},{7,6},{8,7},{9,8},{10,9... | collective-permute-start | bytes 737288 | tf_op jit(solution)/shard_map/ppermute | solution.py:386
  5.0 7.3 %collective-permute-start.1 = (f32[8,128]{1,0:T(8,128)S(1)}, f32[8,128]{1,0:T(8,128)S(1)}, u32[]{:S(2)}, u32[]{:S(2)}) collective-permute-start(f32[8,128]{1,0:T(8,128)S(1)} %get-tuple-element.25), channel_id=1, source_target_pairs={{0,224},{32,0},{64,32},{96,64},{128,96},{160,128},{192,160},{224,1... | collective-permute-start | bytes 12296 | tf_op jit(solution)/shard_map/ppermute | solution.py:386
  12.8 7.0 %collective-permute-start.2 = (f32[1,128]{1,0:T(1,128)S(1)}, f32[1,128]{1,0:T(1,128)S(1)}, u32[]{:S(2)}, u32[]{:S(2)}) collective-permute-start(f32[1,128]{1,0:T(1,128)S(1)} %get-tuple-element.28), channel_id=1, source_target_pairs={{0,1},{1,0},{2,3},{3,2},{4,5},{5,4},{6,7},{7,6},{8,9},{9,8},{10,11... | collective-permute-start | bytes 1544 | tf_op jit(solution)/shard_map/ppermute | solution.py:391
  19.9 3.6 %collective-permute-start.3 = (f32[1,128]{1,0:T(1,128)S(1)}, f32[1,128]{1,0:T(1,128)S(1)}, u32[]{:S(2)}, u32[]{:S(2)}) collective-permute-start(f32[1,128]{1,0:T(1,128)S(1)} %add.6), channel_id=1, source_target_pairs={{0,28},{4,24},{8,20},{12,16},{16,12},{20,8},{24,4},{28,0},{1,29},{... | collective-permute-start | bytes 1544 | tf_op jit(solution)/shard_map/ppermute | solution.py:391
  24.2 14.3 %all-to-all-start = ((f32[64,1,128]{2,1,0:T(1,128)}), f32[64,1,128]{2,1,0:T(1,128)S(1)}, u32[]{:S(2)}, u32[]{:S(2)}) async-start(f32[64,1,128]{2,1,0:T(1,128)} %broadcast_in_dim.9), calls=%async_computation | async-start | bytes 65536 | tf_op jit(solution)/shard_map/all_to_all | solution.py:399

commit v6 on v5

--- a/solution.py
+++ b/solution.py
@@ -55,7 +55,7 @@
     return chosen
 
 
-def operator(depth, level, start, end, target, layers):
+def operator(depth, level, start, end, target, layers, ends=True):
     offset = level - target
     masks = [offset == o for o in (-2, -1, 0, 1, 2)]
     depths = [depth(d) for d in range(-2, 4)]
@@ -78,22 +78,26 @@
     edge2 = second * (linear_second - triple_second)
     mean0 = first * (2.0 * triple_first)
     mean1 = second * (2.0 * triple_second)
-    top, under_top = level == 0, level == 1
-    bottom, over_bottom = level == layers - 2, level == layers - 3
-    e0 = (
-        jnp.where(top | under_top, 0.0, -C1),
-        jnp.where(top, 0.0, jnp.where(under_top, 0.5, C7)),
-        jnp.where(top, 1.5, jnp.where(under_top, 0.5, C7)),
-        jnp.where(top, -0.5, jnp.where(under_top, 0.0, -C1)),
-    )
-    outer = jnp.where(top | bottom, 0.0, -C1)
-    inner = jnp.where(top | bottom, 0.5, C7)
-    e2 = (
-        jnp.where(bottom, -0.5, jnp.where(over_bottom, 0.0, -C1)),
-        jnp.where(bottom, 1.5, jnp.where(over_bottom, 0.5, C7)),
-        jnp.where(bottom, 0.0, jnp.where(over_bottom, 0.5, C7)),
-        jnp.where(bottom | over_bottom, 0.0, -C1),
-    )
+    if ends:
+        top, under_top = level == 0, level == 1
+        bottom, over_bottom = level == layers - 2, level == layers - 3
+        e0 = (
+            jnp.where(top | under_top, 0.0, -C1),
+            jnp.where(top, 0.0, jnp.where(under_top, 0.5, C7)),
+            jnp.where(top, 1.5, jnp.where(under_top, 0.5, C7)),
+            jnp.where(top, -0.5, jnp.where(under_top, 0.0, -C1)),
+        )
+        outer = jnp.where(top | bottom, 0.0, -C1)
+        inner = jnp.where(top | bottom, 0.5, C7)
+        e2 = (
+            jnp.where(bottom, -0.5, jnp.where(over_bottom, 0.0, -C1)),
+            jnp.where(bottom, 1.5, jnp.where(over_bottom, 0.5, C7)),
+            jnp.where(bottom, 0.0, jnp.where(over_bottom, 0.5, C7)),
+            jnp.where(bottom | over_bottom, 0.0, -C1),
+        )
+    else:
+        e0 = e2 = (-C1, C7, C7, -C1)
+        outer, inner = -C1, C7
     taps = {
         -2: e0[0] * edge0,
         -1: e0[1] * edge0 + outer * edge1,
@@ -274,6 +278,7 @@
             row_ref[3, block, :],
             layers_of(k),
             layers,
+            ends=k in (0, layers // STEP - 1),
         )
         zonal = 0.5 * (
             zonal_ref[rows - 1, block, :] + apply_operator(diagonals, shifted(zonal_pad, k))

time: 40.3 us -> 40.3 us (level)
  no operation moved by 1% of the time
where the time goes in v6:
time: 40.3 us; the launch traced here: 39.6 us
  starting transfers between devices  19.1 us (47%)
  waiting for transfers between devices  11.7 us (29%)
  Pallas kernels  7.48 us (19%)
  between operations  0.67 us (2%)
  local copies, waits for them, and re-layouts  0.64 us (2%)
    all_to_all x1, waiting for transfers between devices, sums_to_gather(): return lax.all_to_all(rows, CUBE, 0, 0, tiled=True).reshape(count, 128)  7.96 us
    pallas_call x6, Pallas kernels, kernel(): pl.pallas_call(body, out_shape=tuple((pltpu.VMEM(shape, jnp.float32) if p...  7.48 us
    ppermute x2, starting transfers between devices, add_mirrored(): lax.ppermute(value, axis, [(i, count - 1 - i) for i in range(count)])  6.94 us
    ppermute x2, starting transfers between devices, ring_shift(): lax.ppermute(value, axis, [(i, (i + steps) % count) for i in range(count)])  6.73 us
    all_to_all x1, starting transfers between devices, sums_to_gather(): return lax.all_to_all(rows, CUBE, 0, 0, tiled=True).reshape(count, 128)  5.43 us
    ppermute x2, waiting for transfers between devices, add_mirrored(): lax.ppermute(value, axis, [(i, count - 1 - i) for i in range(count)])  3.72 us
  transfers between devices with their start and end apart: 5, of which 3 were waited for; matrix products, arithmetic and copies ran while one was open for 0% of the time, Pallas kernels for 12%

profile of v6, /device:TPU:1, one launch (start us, length us, event | category | flops | bytes accessed | tf_op | source)
XLA Modules:
  0.0 39.6 jit_solution(7520165540918742414)
XLA Ops:
  0.6 1.2 %shard_map.111 = (f32[4,120,128]{2,1,0:T(8,128)S(1)}, f32[8,128]{1,0:T(8,128)S(1)}) custom-call(f32[2,120,128]{2,1,0:T(8,128)} %depth_ref.3, s32[2,120,128]{2,1,0:T(8,128)} %level_ref.3, bf16[2,120,128]{2,1,0:T(8,128)(2,1)} %start_ref.3, bf16[2,120,128]{2,1,0:T(8,128)(2,1)} %end_ref.3), custom_call_target="tpu_custom_call" | custom-call | flops 100000 | bytes 600000 | tf_op jit(solution)/shard_map/pallas_call | solution.py:414
  1.8 3.2 %collective-permute-start = (f32[4,120,128]{2,1,0:T(8,128)S(1)}, f32[4,120,128]{2,1,0:T(8,128)S(1)}, u32[]{:S(2)}, u32[]{:S(2)}) collective-permute-start(f32[4,120,128]{2,1,0:T(8,128)S(1)} %get-tuple-element.21), channel_id=1, source_target_pairs={{0,31},{1,0},{2,1},{3,2},{4,3},{5,4},{6,5},{7,6},{8,7},{9,8},{10,9... | collective-permute-start | bytes 737288 | tf_op jit(solution)/shard_map/ppermute | solution.py:391
  5.0 3.5 %collective-permute-start.1 = (f32[8,128]{1,0:T(8,128)S(1)}, f32[8,128]{1,0:T(8,128)S(1)}, u32[]{:S(2)}, u32[]{:S(2)}) collective-permute-start(f32[8,128]{1,0:T(8,128)S(1)} %get-tuple-element.25), channel_id=1, source_target_pairs={{0,224},{32,0},{64,32},{96,64},{128,96},{160,128},{192,160},{224,1... | collective-permute-start | bytes 12296 | tf_op jit(solution)/shard_map/ppermute | solution.py:391
  8.5 3.8 %shard_map.112 = (f32[8,2,120,128]{3,2,1,0:T(8,128)S(1)}, f32[2,120,128]{2,1,0:T(8,128)S(1)}, f32[2,120,128]{2,1,0:T(8,128)S(1)}, f32[2,120,128]{2,1,0:T(8,128)S...) custom-call(bf16[8,2,120,128]{3,2,1,0:T(8,128)(2,1)} %species_ref.1, ...), custom_call_target="tpu_custom_call" | custom-call | flops 20000000 | bytes 2000000 | tf_op jit(solution)/shard_map/pallas_call | solution.py:414
  12.3 0.0 collective-permute-done.1.column_ref
  12.3 0.1 shard_map.113
  12.4 0.0 collective-permute-done.row_ref
  12.4 0.4 shard_map.114
  12.8 6.2 %collective-permute-start.2 = (f32[1,128]{1,0:T(1,128)S(1)}, f32[1,128]{1,0:T(1,128)S(1)}, u32[]{:S(2)}, u32[]{:S(2)}) collective-permute-start(f32[1,128]{1,0:T(1,128)S(1)} %get-tuple-element.28), channel_id=1, source_target_pairs={{0,1},{1,0},{2,3},{3,2},{4,5},{5,4},{6,7},{7,6},{8,9},{9,8},{10,11... | collective-permute-start | bytes 1544 | tf_op jit(solution)/shard_map/ppermute | solution.py:396
  19.0 0.8 %collective-permute-done.2 = f32[1,128]{1,0:T(1,128)S(1)} collective-permute-done((f32[1,128]{1,0:T(1,128)S(1)}, f32[1,128]{1,0:T(1,128)S(1)}, u32[]{:S(2)}, u32[]{:S(2)}) %collective-permute-start.2) | collective-permute-done | bytes 544 | tf_op jit(solution)/shard_map/ppermute | solution.py:396
  19.9 0.7 %collective-permute-start.3 = (f32[1,128]{1,0:T(1,128)S(1)}, f32[1,128]{1,0:T(1,128)S(1)}, u32[]{:S(2)}, u32[]{:S(2)}) collective-permute-start(f32[1,128]{1,0:T(1,128)S(1)} %add.6), channel_id=1, source_target_pairs={{0,28},{4,24},{8,20},{12,16},{16,12},{20,8},{24,4},{28,0},{1,29},{... | collective-permute-start | bytes 1544 | tf_op jit(solution)/shard_map/ppermute | solution.py:396
  20.6 2.9 %collective-permute-done.3 = f32[1,128]{1,0:T(1,128)S(1)} collective-permute-done((f32[1,128]{1,0:T(1,128)S(1)}, f32[1,128]{1,0:T(1,128)S(1)}, u32[]{:S(2)}, u32[]{:S(2)}) %collective-permute-start.3) | collective-permute-done | bytes 544 | tf_op jit(solution)/shard_map/ppermute | solution.py:396
  23.5 0.6 %broadcast_in_dim.9 = f32[64,1,128]{2,1,0:T(1,128)} broadcast(f32[128]{0:T(128)S(1)} %add_bitcast_fusion), dimensions={2} | broadcast | bytes 33280 | tf_op jit(solution)/shard_map/broadcast_in_dim | solution.py:403
  24.1 5.4 %all-to-all-start = ((f32[64,1,128]{2,1,0:T(1,128)}), f32[64,1,128]{2,1,0:T(1,128)S(1)}, u32[]{:S(2)}, u32[]{:S(2)}) async-start(f32[64,1,128]{2,1,0:T(1,128)} %broadcast_in_dim.9), calls=%async_computation | async-start | bytes 65536 | tf_op jit(solution)/shard_map/all_to_all | solution.py:404
  29.6 0.9 %shard_map.116 = (f32[2,120,128]{2,1,0:T(8,128)}, f32[2,120,128]{2,1,0:T(8,128)}) custom-call(f32[2,120,128]{2,1,0:T(8,128)S(1)} %get-tuple-element.22.zonal_ref, f32[120,128]{1,0:T(8,128)S(1)} %get-tuple-element.32.last_ref, f32[2,120,128]{2,1,0:T(8,128)S(1)} %get-tuple-element.33.merid_ref, f32[8,128]{1,0:T(8,128)S(1)} %get-tuple-element.34.edge_ref), custom_call_target="tpu_custom_call" | custom-call | flops 200000 | bytes 700000 | tf_op jit(solution)/shard_map/pallas_call | solution.py:414
  30.4 8.0 %all-to-all-done = f32[64,1,128]{2,1,0:T(1,128)S(1)} async-done(((f32[64,1,128]{2,1,0:T(1,128)}), f32[64,1,128]{2,1,0:T(1,128)S(1)}, u32[]{:S(2)}, u32[]{:S(2)}) %all-to-all-start) | async-done | bytes 32800 | tf_op jit(solution)/shard_map/all_to_all | solution.py:404
  38.4 1.2 %shard_map.115 = (f32[8,2,120,128]{3,2,1,0:T(8,128)}, f32[2,120,128]{2,1,0:T(8,128)}) custom-call(f32[64,128]{1,0:T(8,128)S(1)} %bitcast.3, f32[8,2,120,128]{3,2,1,0:T(8,128)S(1)} %get-tuple-element.29.tracer_ref, f32[2,120,128]{2,1,0:T(8,128)S(1)} %get-tuple-element.30.warmth_ref), custom_call_target="tpu_custom_call" | custom-call | flops 1000000 | bytes 2000000 | tf_op jit(solution)/shard_map/pallas_call | solution.py:414
  (2 shorter events, 0.0 us)
Async XLA Ops:
  1.8 10.6 %collective-permute-start = (f32[4,120,128]{2,1,0:T(8,128)S(1)}, f32[4,120,128]{2,1,0:T(8,128)S(1)}, u32[]{:S(2)}, u32[]{:S(2)}) collective-permute-start(f32[4,120,128]{2,1,0:T(8,128)S(1)} %get-tuple-element.21), channel_id=1, source_target_pairs={{0,31},{1,0},{2,1},{3,2},{4,3},{5,4},{6,5},{7,6},{8,7},{9,8},{10,9... | collective-permute-start | bytes 737288 | tf_op jit(solution)/shard_map/ppermute | solution.py:391
  5.0 7.3 %collective-permute-start.1 = (f32[8,128]{1,0:T(8,128)S(1)}, f32[8,128]{1,0:T(8,128)S(1)}, u32[]{:S(2)}, u32[]{:S(2)}) collective-permute-start(f32[8,128]{1,0:T(8,128)S(1)} %get-tuple-element.25), channel_id=1, source_target_pairs={{0,224},{32,0},{64,32},{96,64},{128,96},{160,128},{192,160},{224,1... | collective-permute-start | bytes 12296 | tf_op jit(solution)/shard_map/ppermute | solution.py:391
  12.8 7.0 %collective-permute-start.2 = (f32[1,128]{1,0:T(1,128)S(1)}, f32[1,128]{1,0:T(1,128)S(1)}, u32[]{:S(2)}, u32[]{:S(2)}) collective-permute-start(f32[1,128]{1,0:T(1,128)S(1)} %get-tuple-element.28), channel_id=1, source_target_pairs={{0,1},{1,0},{2,3},{3,2},{4,5},{5,4},{6,7},{7,6},{8,9},{9,8},{10,11... | collective-permute-start | bytes 1544 | tf_op jit(solution)/shard_map/ppermute | solution.py:396
  19.9 3.6 %collective-permute-start.3 = (f32[1,128]{1,0:T(1,128)S(1)}, f32[1,128]{1,0:T(1,128)S(1)}, u32[]{:S(2)}, u32[]{:S(2)}) collective-permute-start(f32[1,128]{1,0:T(1,128)S(1)} %add.6), channel_id=1, source_target_pairs={{0,28},{4,24},{8,20},{12,16},{16,12},{20,8},{24,4},{28,0},{1,29},{... | collective-permute-start | bytes 1544 | tf_op jit(solution)/shard_map/ppermute | solution.py:396
  24.1 14.3 %all-to-all-start = ((f32[64,1,128]{2,1,0:T(1,128)}), f32[64,1,128]{2,1,0:T(1,128)S(1)}, u32[]{:S(2)}, u32[]{:S(2)}) async-start(f32[64,1,128]{2,1,0:T(1,128)} %broadcast_in_dim.9), calls=%async_computation | async-start | bytes 65536 | tf_op jit(solution)/shard_map/all_to_all | solution.py:404

commit v7 on v6

--- a/solution.py
+++ b/solution.py
@@ -368,7 +368,7 @@
 
 
 def correct_body(gathered_ref, tracer_ref, warmth_ref, tracers_out, warmth_out, new_s, heat_s, sem):
-    tracers = tracer_ref.shape[0]
+    tracers, rows = tracer_ref.shape[:2]
     totals = jnp.sum(gathered_ref[...], axis=0, keepdims=True)
     spread = [
         jnp.broadcast_to(totals[:, i : i + 1], (1, 128)) for i in range(tracers + 2)
@@ -376,11 +376,16 @@
     scale = 1.0 / spread[tracers + 1]
     copies = []
     for t in range(tracers):
-        new_s[t] = tracer_ref[t] + spread[t] * scale
-        copies.append(pltpu.make_async_copy(new_s.at[t], tracers_out.at[t], sem.at[t]))
-        copies[-1].start()
+        for r in range(rows):
+            new_s[t, r] = tracer_ref[t, r] + spread[t] * scale
+            copies.append(
+                pltpu.make_async_copy(
+                    new_s.at[t, r], tracers_out.at[t, r], sem.at[t * rows + r]
+                )
+            )
+            copies[-1].start()
     heat_s[...] = warmth_ref[...] + spread[tracers] * (scale * (1.0 / HEAT))
-    copies.append(pltpu.make_async_copy(heat_s, warmth_out, sem.at[tracers]))
+    copies.append(pltpu.make_async_copy(heat_s, warmth_out, sem.at[tracers * rows]))
     copies[-1].start()
     for copy in copies:
         copy.wait()
@@ -502,7 +507,7 @@
         correct_body,
         1_000_000,
         2_000_000,
-        [real((tracers, *plane)), real(plane), pltpu.SemaphoreType.DMA((tracers + 1,))],
+        [real((tracers, *plane)), real(plane), pltpu.SemaphoreType.DMA((tracers * rows + 1,))],
         range(3),
         [((tracers, *plane), "any"), (plane, "any")],
         (gathered, tracer_new, warmth_new),

time: 40.3 us -> 40.3 us (level)
  no operation moved by 1% of the time
where the time goes in v7:
time: 40.3 us; the launch traced here: 39.6 us
  starting transfers between devices  19.1 us (47%)
  waiting for transfers between devices  11.7 us (29%)
  Pallas kernels  7.54 us (19%)
  between operations  0.67 us (2%)
  local copies, waits for them, and re-layouts  0.64 us (2%)
    all_to_all x1, waiting for transfers between devices, sums_to_gather(): return lax.all_to_all(rows, CUBE, 0, 0, tiled=True).reshape(count, 128)  7.96 us
    pallas_call x6, Pallas kernels, kernel(): pl.pallas_call(body, out_shape=tuple((pltpu.VMEM(shape, jnp.float32) if p...  7.54 us
    ppermute x2, starting transfers between devices, add_mirrored(): lax.ppermute(value, axis, [(i, count - 1 - i) for i in range(count)])  6.94 us
    ppermute x2, starting transfers between devices, ring_shift(): lax.ppermute(value, axis, [(i, (i + steps) % count) for i in range(count)])  6.73 us
    all_to_all x1, starting transfers between devices, sums_to_gather(): return lax.all_to_all(rows, CUBE, 0, 0, tiled=True).reshape(count, 128)  5.43 us
    ppermute x2, waiting for transfers between devices, add_mirrored(): lax.ppermute(value, axis, [(i, count - 1 - i) for i in range(count)])  3.72 us
  transfers between devices with their start and end apart: 5, of which 3 were waited for; matrix products, arithmetic and copies ran while one was open for 0% of the time, Pallas kernels for 12%

profile of v7, /device:TPU:1, one launch (start us, length us, event | category | flops | bytes accessed | tf_op | source)
XLA Modules:
  0.0 39.6 jit_solution(733295666124228319)
XLA Ops:
  0.6 1.2 %shard_map.111 = (f32[4,120,128]{2,1,0:T(8,128)S(1)}, f32[8,128]{1,0:T(8,128)S(1)}) custom-call(f32[2,120,128]{2,1,0:T(8,128)} %depth_ref.3, s32[2,120,128]{2,1,0:T(8,128)} %level_ref.3, bf16[2,120,128]{2,1,0:T(8,128)(2,1)} %start_ref.3, bf16[2,120,128]{2,1,0:T(8,128)(2,1)} %end_ref.3), custom_call_target="tpu_custom_call" | custom-call | flops 100000 | bytes 600000 | tf_op jit(solution)/shard_map/pallas_call | solution.py:419
  1.8 3.2 %collective-permute-start = (f32[4,120,128]{2,1,0:T(8,128)S(1)}, f32[4,120,128]{2,1,0:T(8,128)S(1)}, u32[]{:S(2)}, u32[]{:S(2)}) collective-permute-start(f32[4,120,128]{2,1,0:T(8,128)S(1)} %get-tuple-element.21), channel_id=1, source_target_pairs={{0,31},{1,0},{2,1},{3,2},{4,3},{5,4},{6,5},{7,6},{8,7},{9,8},{10,9... | collective-permute-start | bytes 737288 | tf_op jit(solution)/shard_map/ppermute | solution.py:396
  5.0 3.5 %collective-permute-start.1 = (f32[8,128]{1,0:T(8,128)S(1)}, f32[8,128]{1,0:T(8,128)S(1)}, u32[]{:S(2)}, u32[]{:S(2)}) collective-permute-start(f32[8,128]{1,0:T(8,128)S(1)} %get-tuple-element.25), channel_id=1, source_target_pairs={{0,224},{32,0},{64,32},{96,64},{128,96},{160,128},{192,160},{224,1... | collective-permute-start | bytes 12296 | tf_op jit(solution)/shard_map/ppermute | solution.py:396
  8.5 3.8 %shard_map.112 = (f32[8,2,120,128]{3,2,1,0:T(8,128)S(1)}, f32[2,120,128]{2,1,0:T(8,128)S(1)}, f32[2,120,128]{2,1,0:T(8,128)S(1)}, f32[2,120,128]{2,1,0:T(8,128)S...) custom-call(bf16[8,2,120,128]{3,2,1,0:T(8,128)(2,1)} %species_ref.1, ...), custom_call_target="tpu_custom_call" | custom-call | flops 20000000 | bytes 2000000 | tf_op jit(solution)/shard_map/pallas_call | solution.py:419
  12.3 0.0 collective-permute-done.1.column_ref
  12.3 0.1 shard_map.113
  12.4 0.0 collective-permute-done.row_ref
  12.4 0.4 shard_map.114
  12.8 6.2 %collective-permute-start.2 = (f32[1,128]{1,0:T(1,128)S(1)}, f32[1,128]{1,0:T(1,128)S(1)}, u32[]{:S(2)}, u32[]{:S(2)}) collective-permute-start(f32[1,128]{1,0:T(1,128)S(1)} %get-tuple-element.28), channel_id=1, source_target_pairs={{0,1},{1,0},{2,3},{3,2},{4,5},{5,4},{6,7},{7,6},{8,9},{9,8},{10,11... | collective-permute-start | bytes 1544 | tf_op jit(solution)/shard_map/ppermute | solution.py:401
  19.0 0.8 %collective-permute-done.2 = f32[1,128]{1,0:T(1,128)S(1)} collective-permute-done((f32[1,128]{1,0:T(1,128)S(1)}, f32[1,128]{1,0:T(1,128)S(1)}, u32[]{:S(2)}, u32[]{:S(2)}) %collective-permute-start.2) | collective-permute-done | bytes 544 | tf_op jit(solution)/shard_map/ppermute | solution.py:401
  19.9 0.7 %collective-permute-start.3 = (f32[1,128]{1,0:T(1,128)S(1)}, f32[1,128]{1,0:T(1,128)S(1)}, u32[]{:S(2)}, u32[]{:S(2)}) collective-permute-start(f32[1,128]{1,0:T(1,128)S(1)} %add.6), channel_id=1, source_target_pairs={{0,28},{4,24},{8,20},{12,16},{16,12},{20,8},{24,4},{28,0},{1,29},{... | collective-permute-start | bytes 1544 | tf_op jit(solution)/shard_map/ppermute | solution.py:401
  20.6 2.9 %collective-permute-done.3 = f32[1,128]{1,0:T(1,128)S(1)} collective-permute-done((f32[1,128]{1,0:T(1,128)S(1)}, f32[1,128]{1,0:T(1,128)S(1)}, u32[]{:S(2)}, u32[]{:S(2)}) %collective-permute-start.3) | collective-permute-done | bytes 544 | tf_op jit(solution)/shard_map/ppermute | solution.py:401
  23.5 0.6 %broadcast_in_dim.9 = f32[64,1,128]{2,1,0:T(1,128)} broadcast(f32[128]{0:T(128)S(1)} %add_bitcast_fusion), dimensions={2} | broadcast | bytes 33280 | tf_op jit(solution)/shard_map/broadcast_in_dim | solution.py:408
  24.1 5.4 %all-to-all-start = ((f32[64,1,128]{2,1,0:T(1,128)}), f32[64,1,128]{2,1,0:T(1,128)S(1)}, u32[]{:S(2)}, u32[]{:S(2)}) async-start(f32[64,1,128]{2,1,0:T(1,128)} %broadcast_in_dim.9), calls=%async_computation | async-start | bytes 65536 | tf_op jit(solution)/shard_map/all_to_all | solution.py:409
  29.6 0.9 %shard_map.116 = (f32[2,120,128]{2,1,0:T(8,128)}, f32[2,120,128]{2,1,0:T(8,128)}) custom-call(f32[2,120,128]{2,1,0:T(8,128)S(1)} %get-tuple-element.22.zonal_ref, f32[120,128]{1,0:T(8,128)S(1)} %get-tuple-element.32.last_ref, f32[2,120,128]{2,1,0:T(8,128)S(1)} %get-tuple-element.33.merid_ref, f32[8,128]{1,0:T(8,128)S(1)} %get-tuple-element.34.edge_ref), custom_call_target="tpu_custom_call" | custom-call | flops 200000 | bytes 700000 | tf_op jit(solution)/shard_map/pallas_call | solution.py:419
  30.4 8.0 %all-to-all-done = f32[64,1,128]{2,1,0:T(1,128)S(1)} async-done(((f32[64,1,128]{2,1,0:T(1,128)}), f32[64,1,128]{2,1,0:T(1,128)S(1)}, u32[]{:S(2)}, u32[]{:S(2)}) %all-to-all-start) | async-done | bytes 32800 | tf_op jit(solution)/shard_map/all_to_all | solution.py:409
  38.4 1.2 %shard_map.115 = (f32[8,2,120,128]{3,2,1,0:T(8,128)}, f32[2,120,128]{2,1,0:T(8,128)}) custom-call(f32[64,128]{1,0:T(8,128)S(1)} %bitcast.3, f32[8,2,120,128]{3,2,1,0:T(8,128)S(1)} %get-tuple-element.29.tracer_ref, f32[2,120,128]{2,1,0:T(8,128)S(1)} %get-tuple-element.30.warmth_ref), custom_call_target="tpu_custom_call" | custom-call | flops 1000000 | bytes 2000000 | tf_op jit(solution)/shard_map/pallas_call | solution.py:419
  (2 shorter events, 0.0 us)
Async XLA Ops:
  1.8 10.6 %collective-permute-start = (f32[4,120,128]{2,1,0:T(8,128)S(1)}, f32[4,120,128]{2,1,0:T(8,128)S(1)}, u32[]{:S(2)}, u32[]{:S(2)}) collective-permute-start(f32[4,120,128]{2,1,0:T(8,128)S(1)} %get-tuple-element.21), channel_id=1, source_target_pairs={{0,31},{1,0},{2,1},{3,2},{4,3},{5,4},{6,5},{7,6},{8,7},{9,8},{10,9... | collective-permute-start | bytes 737288 | tf_op jit(solution)/shard_map/ppermute | solution.py:396
  5.0 7.3 %collective-permute-start.1 = (f32[8,128]{1,0:T(8,128)S(1)}, f32[8,128]{1,0:T(8,128)S(1)}, u32[]{:S(2)}, u32[]{:S(2)}) collective-permute-start(f32[8,128]{1,0:T(8,128)S(1)} %get-tuple-element.25), channel_id=1, source_target_pairs={{0,224},{32,0},{64,32},{96,64},{128,96},{160,128},{192,160},{224,1... | collective-permute-start | bytes 12296 | tf_op jit(solution)/shard_map/ppermute | solution.py:396
  12.8 7.0 %collective-permute-start.2 = (f32[1,128]{1,0:T(1,128)S(1)}, f32[1,128]{1,0:T(1,128)S(1)}, u32[]{:S(2)}, u32[]{:S(2)}) collective-permute-start(f32[1,128]{1,0:T(1,128)S(1)} %get-tuple-element.28), channel_id=1, source_target_pairs={{0,1},{1,0},{2,3},{3,2},{4,5},{5,4},{6,7},{7,6},{8,9},{9,8},{10,11... | collective-permute-start | bytes 1544 | tf_op jit(solution)/shard_map/ppermute | solution.py:401
  19.9 3.6 %collective-permute-start.3 = (f32[1,128]{1,0:T(1,128)S(1)}, f32[1,128]{1,0:T(1,128)S(1)}, u32[]{:S(2)}, u32[]{:S(2)}) collective-permute-start(f32[1,128]{1,0:T(1,128)S(1)} %add.6), channel_id=1, source_target_pairs={{0,28},{4,24},{8,20},{12,16},{16,12},{20,8},{24,4},{28,0},{1,29},{... | collective-permute-start | bytes 1544 | tf_op jit(solution)/shard_map/ppermute | solution.py:401
  24.1 14.3 %all-to-all-start = ((f32[64,1,128]{2,1,0:T(1,128)}), f32[64,1,128]{2,1,0:T(1,128)S(1)}, u32[]{:S(2)}, u32[]{:S(2)}) async-start(f32[64,1,128]{2,1,0:T(1,128)} %broadcast_in_dim.9), calls=%async_computation | async-start | bytes 65536 | tf_op jit(solution)/shard_map/all_to_all | solution.py:409
